TPU v7x, 32 devices: a whole 2x2x4 slice. The times are simulated.
32 devices in a mesh: rows: 8 (over y, x, core), seq: 4 (over z).
Axes of the slice: x: 2, y: 2, z: 4, core: 2. Of those that a mesh axis runs over, the one named last changes fastest.
Arguments:
- tokens: bfloat16 [8, 1024, 512], P('rows', 'seq'), may hold values from -6 to 6
- segment_ids: int32 [8, 1024], P('rows', 'seq'), may hold values from 0 to 3, as said below
- prenorm_gain: float32 [512], replicated, may hold values from 0.5 to 1.5
- prenorm_shift: float32 [512], replicated, may hold values from -3 to 3
- query_proj: bfloat16 [512, 512], replicated, may hold values from -1 to 1
- query_bias: float32 [512], replicated, may hold values from -3 to 3
- key_proj: bfloat16 [512, 512], replicated, may hold values from -1 to 1
- value_proj: bfloat16 [512, 512], replicated, may hold values from -0.25 to 0.25
- value_bias: float32 [512], replicated, may hold values from -3 to 3
- output_proj: bfloat16 [512, 512], replicated, may hold values from -1 to 1
- output_bias: float32 [512], replicated, may hold values from -3 to 3
- midnorm_gain: float32 [512], replicated, may hold values from 0.5 to 1.5
- midnorm_shift: float32 [512], replicated, may hold values from -3 to 3
- inner_proj: bfloat16 [512, 2048], replicated, may hold values from -0.25 to 0.25
- inner_bias: float32 [2048], replicated, may hold values from -3 to 3
- outer_proj: bfloat16 [2048, 512], replicated, may hold values from -0.125 to 0.125
- outer_bias: float32 [512], replicated, may hold values from -3 to 3
- upstream: bfloat16 [8, 1024, 512], P('rows', 'seq'), may hold values from -6 to 6
Outputs:
- layer_output: bfloat16 [8, 1024, 512], P('rows', 'seq')
- input_grad: bfloat16 [8, 1024, 512], P('rows', 'seq')
- prenorm_gain_gradient: float32 [512], replicated
- prenorm_shift_gradient: float32 [512], replicated
- query_grad: float32 [512, 512], replicated
- querybias_grad: float32 [512], replicated
- key_grad: float32 [512, 512], replicated
- value_grad: float32 [512, 512], replicated
- valuebias_grad: float32 [512], replicated
- output_grad: float32 [512, 512], replicated
- outputbias_grad: float32 [512], replicated
- midgain_grad: float32 [512], replicated
- midshift_grad: float32 [512], replicated
- inner_grad: float32 [512, 2048], replicated
- innerbias_grad: float32 [2048], replicated
- outer_grad: float32 [2048, 512], replicated
- outerbias_grad: float32 [512], replicated
Inputs may be any that keep to these rules, and one draw needn't show every extreme that they name: `segment_ids`: in each row the ids never fall until a tail of 1 to 128 padding positions with id 0; the last position before the tail has id 3.
All inputs are finite; a program needn't handle non-finite values.
Results may differ from a plain program's by a relative error of at most 0.011.
Values may be sent and summed in bfloat16 or wider, within the bound.
A program may use at most 128 MiB of HBM per device.

v0:
```python
from functools import reduce
import math

import jax
import jax.numpy as jnp
from jax import lax
from jax.sharding import PartitionSpec as P

HEADS = 8
HEAD_DIM = 64
NR = 16


LOG_TWO = math.log(2.0)
EPSILON = 1e-05


def with_halo(block, sides, width):
    for axis, dim in sides:
        count = lax.axis_size(axis)
        forward = [(i, i + 1) for i in range(count - 1)]
        backward = [(target, source) for source, target in forward]
        low = lax.ppermute(
            lax.slice_in_dim(block, block.shape[dim] - width, None, axis=dim), axis, forward
        )
        high = lax.ppermute(lax.slice_in_dim(block, 0, width, axis=dim), axis, backward)
        block = jnp.concatenate([low, block, high], axis=dim)
    return block


def normalize(values, gain, shift):
    center = values - jnp.mean(values, axis=-1, keepdims=True)
    spread = jnp.mean(center * center, axis=-1, keepdims=True)
    return center * lax.rsqrt(spread + EPSILON) * gain + shift


def gelu_tanh(values):
    return jax.nn.gelu(values, approximate=True)


def crossprod(left, right):
    return lax.dot_general(
        left, right, (((0,), (0,)), ((), ())), preferred_element_type=jnp.float32
    )


def backprod(left, right):
    return lax.dot_general(
        left, right, (((1,), (1,)), ((), ())), preferred_element_type=jnp.float32
    )


def level_windows(padded, count):
    level_depth = padded.shape[0]
    window_width = padded.shape[2]
    before = padded[:, : count * NR].reshape(level_depth, count, NR, window_width)
    middle = padded[:, NR : NR + count * NR].reshape(level_depth, count, NR, window_width)
    after = padded[:, 2 * NR : 2 * NR + count * NR].reshape(level_depth, count, NR, window_width)
    return jnp.concatenate([before, middle, after], axis=2)


def fold_windows(grads, count):
    level_depth = grads.shape[0]
    window_width = grads.shape[3]
    part_before = grads[:, :, :NR].reshape(level_depth, count * NR, window_width)
    part_middle = grads[:, :, NR : 2 * NR].reshape(level_depth, count * NR, window_width)
    part_after = grads[:, :, 2 * NR :].reshape(level_depth, count * NR, window_width)
    return (
        jnp.pad(part_before, ((0, 0), (0, 2 * NR), (0, 0)))
        + jnp.pad(part_middle, ((0, 0), (NR, NR), (0, 0)))
        + jnp.pad(part_after, ((0, 0), (2 * NR, 0), (0, 0)))
    )


def level_mask(level, start, window_span, segments, coarse_ids):
    block = NR * 2**level
    coarse_count = coarse_ids.shape[1]
    positions = start + jnp.arange(window_span, dtype=jnp.int32)
    offsets = jnp.arange(3 * NR, dtype=jnp.int32)
    key_index = (positions // block - 1)[:, None] * NR + offsets[None, :]
    valid = (key_index >= 0) & (key_index < coarse_count)
    key_ids = jnp.take(coarse_ids, jnp.clip(key_index, 0, coarse_count - 1), axis=1)
    mask = valid[None] & (key_ids == segments[:, :, None])
    if level > 0:
        distant = jnp.abs(key_index // (NR // 2) - (positions // (block // 2))[:, None]) > 1
        mask = mask & (key_ids != 0) & distant[None]
    return mask[:, :, None, :]


def level_scores(query_blocks, key_window, level, level_depth, window_span):
    raw = jnp.einsum(
        "rbqhd,rbkhd->rbqhk", query_blocks, key_window, preferred_element_type=jnp.float32
    )
    return (
        raw.reshape(level_depth, window_span, HEADS, 3 * NR) * (1.0 / math.sqrt(HEAD_DIM))
        + level * LOG_TWO
    )


def shards(
    tokens,
    segment_ids,
    prenorm_gain,
    prenorm_shift,
    query_proj,
    query_bias,
    key_proj,
    value_proj,
    value_bias,
    output_proj,
    output_bias,
    midnorm_gain,
    midnorm_shift,
    inner_proj,
    inner_bias,
    outer_proj,
    outer_bias,
    upstream,
):
    level_depth, window_span, window_width = tokens.shape
    flat = level_depth * window_span
    seq_count = lax.axis_size("seq")
    length = window_span * seq_count
    near = (window_span // NR).bit_length() - 1
    top = (length // NR).bit_length() - 2
    start = lax.axis_index("seq") * window_span
    scale = 1.0 / math.sqrt(HEAD_DIM)
    token_f = tokens.astype(jnp.float32)
    normed, first_pullback = jax.vjp(normalize, token_f, prenorm_gain, prenorm_shift)
    first = normed.astype(jnp.bfloat16).reshape(flat, window_width)
    query = (jnp.dot(first, query_proj, preferred_element_type=jnp.float32) + query_bias).astype(
        jnp.bfloat16
    )
    keys = jnp.dot(first, key_proj, preferred_element_type=jnp.float32).astype(jnp.bfloat16)
    values = (jnp.dot(first, value_proj, preferred_element_type=jnp.float32) + value_bias).astype(
        jnp.bfloat16
    )
    base_pairs = jnp.concatenate([keys, values], axis=1).reshape(
        level_depth, window_span, 2 * window_width
    )
    coarse = [base_pairs]
    current = base_pairs.astype(jnp.float32)
    for level in range(1, top + 1):
        halves = current.reshape(level_depth, current.shape[1] // 2, 2, 2 * window_width)
        current = 0.5 * (halves[:, :, 0] + halves[:, :, 1])
        coarse.append(current.astype(jnp.bfloat16))
    padded = [with_halo(coarse[level], (("seq", 1),), NR) for level in range(near + 1)]
    far_levels = list(range(near + 1, top + 1))
    far_local = jnp.concatenate([coarse[level] for level in far_levels], axis=1)
    far_total = far_local.shape[1]
    gathered, row_segments = (
        lax.all_gather(far_local, "seq", axis=1, tiled=True),
        lax.all_gather(segment_ids.astype(jnp.bfloat16), "seq", axis=1, tiled=True),
    )
    row_segments = row_segments.astype(jnp.int32)
    grouped = gathered.reshape(level_depth, seq_count, far_total, 2 * window_width)
    offset = 0
    for level in far_levels:
        local_count = window_span // 2**level
        whole = grouped[:, :, offset : offset + local_count].reshape(
            level_depth, seq_count * local_count, 2 * window_width
        )
        padded.append(jnp.pad(whole, ((0, 0), (NR, NR), (0, 0))))
        offset += local_count
    level_ids = [row_segments]
    for level in range(1, top + 1):
        halves_ids = level_ids[-1].reshape(level_depth, -1, 2)
        level_ids.append(
            jnp.where(halves_ids[:, :, 0] == halves_ids[:, :, 1], halves_ids[:, :, 0], 0)
        )
    heads_query = query.reshape(level_depth, window_span, HEADS, HEAD_DIM)
    level_info = []
    maskeds = []
    for level in range(top + 1):
        block = NR * 2**level
        if level <= near:
            count = window_span // block
            window = level_windows(padded[level], count)
        else:
            count = 1
            corner = start // block * NR
            window = lax.dynamic_slice_in_dim(padded[level], corner, 3 * NR, axis=1)[:, None]
        query_len = window_span // count
        query_blocks = heads_query.reshape(level_depth, count, query_len, HEADS, HEAD_DIM)
        key_window = window[..., :window_width].reshape(level_depth, count, 3 * NR, HEADS, HEAD_DIM)
        value_window = window[..., window_width:].reshape(
            level_depth, count, 3 * NR, HEADS, HEAD_DIM
        )
        mask = level_mask(level, start, window_span, segment_ids, level_ids[level])
        score = level_scores(query_blocks, key_window, level, level_depth, window_span)
        maskeds.append(jnp.where(mask, score, -1e30))
        level_info.append((count, query_blocks, key_window, value_window, mask))
    peak = reduce(jnp.maximum, [jnp.max(item, axis=3) for item in maskeds])
    total = jnp.zeros((level_depth, window_span, HEADS), jnp.float32)
    for level in range(top + 1):
        total = total + jnp.sum(
            jnp.where(level_info[level][4], jnp.exp(maskeds[level] - peak[..., None]), 0.0), axis=3
        )
    norm_log = (peak + jnp.log(total))[..., None]
    accum = jnp.zeros((level_depth, window_span, HEADS, HEAD_DIM), jnp.float32)
    for level in range(top + 1):
        count, query_blocks, key_window, value_window, mask = level_info[level]
        prob = jnp.where(mask, jnp.exp(maskeds[level] - norm_log), 0.0).astype(jnp.bfloat16)
        part = prob.reshape(level_depth, count, window_span // count, HEADS, 3 * NR)
        mixed = jnp.einsum(
            "rbqhk,rbkhd->rbqhd", part, value_window, preferred_element_type=jnp.float32
        )
        accum = accum + mixed.reshape(level_depth, window_span, HEADS, HEAD_DIM)
    attended = accum.reshape(flat, window_width).astype(jnp.bfloat16)
    branch = jnp.dot(attended, output_proj, preferred_element_type=jnp.float32) + output_bias
    mid = token_f + branch.reshape(level_depth, window_span, window_width)
    normed_mid, pull_second = jax.vjp(normalize, mid, midnorm_gain, midnorm_shift)
    second = normed_mid.astype(jnp.bfloat16).reshape(flat, window_width)
    pre = jnp.dot(second, inner_proj, preferred_element_type=jnp.float32) + inner_bias
    act_f, pull_gelu = jax.vjp(gelu_tanh, pre)
    act = act_f.astype(jnp.bfloat16)
    result = mid + (
        jnp.dot(act, outer_proj, preferred_element_type=jnp.float32) + outer_bias
    ).reshape(level_depth, window_span, window_width)
    layer_output = result.astype(jnp.bfloat16)
    grad_flat = upstream.reshape(flat, window_width)
    outer_grad = crossprod(act, grad_flat)
    outerbias_grad = jnp.sum(grad_flat.astype(jnp.float32), axis=0)
    d_act = backprod(grad_flat, outer_proj)
    d_pre = pull_gelu(d_act)[0].astype(jnp.bfloat16)
    inner_grad = crossprod(second, d_pre)
    innerbias_grad = jnp.sum(d_pre.astype(jnp.float32), axis=0)
    d_second = backprod(d_pre, inner_proj)
    d_mid_norm, midgain_grad, midshift_grad = pull_second(
        d_second.reshape(level_depth, window_span, window_width)
    )
    d_mid = upstream.astype(jnp.float32) + d_mid_norm
    d_branch = d_mid.reshape(flat, window_width).astype(jnp.bfloat16)
    output_grad = crossprod(attended, d_branch)
    outputbias_grad = jnp.sum(d_branch.astype(jnp.float32), axis=0)
    d_attended = backprod(d_branch, output_proj).astype(jnp.bfloat16)
    attended_heads = d_attended.reshape(level_depth, window_span, HEADS, HEAD_DIM)
    probs = []
    dprobs = []
    delta = jnp.zeros((level_depth, window_span, HEADS), jnp.float32)
    for level in range(top + 1):
        count, query_blocks, key_window, value_window, mask = level_info[level]
        score = level_scores(query_blocks, key_window, level, level_depth, window_span)
        prob = jnp.where(mask, jnp.exp(jnp.where(mask, score, -1e30) - norm_log), 0.0)
        grad_blocks = attended_heads.reshape(
            level_depth, count, window_span // count, HEADS, HEAD_DIM
        )
        dprob = jnp.einsum(
            "rbqhd,rbkhd->rbqhk", grad_blocks, value_window, preferred_element_type=jnp.float32
        )
        dprob = dprob.reshape(level_depth, window_span, HEADS, 3 * NR)
        delta = delta + jnp.sum(prob * dprob, axis=3)
        probs.append(prob)
        dprobs.append(dprob)
    d_query = jnp.zeros((level_depth, window_span, HEADS, HEAD_DIM), jnp.float32)
    level_grads = []
    for level in range(top + 1):
        count, query_blocks, key_window, value_window, mask = level_info[level]
        query_len = window_span // count
        grad_blocks = attended_heads.reshape(level_depth, count, query_len, HEADS, HEAD_DIM)
        d_score = probs[level] * (dprobs[level] - delta[..., None])
        d_raw = (
            (d_score * scale)
            .astype(jnp.bfloat16)
            .reshape(level_depth, count, query_len, HEADS, 3 * NR)
        )
        gathered_query = jnp.einsum(
            "rbqhk,rbkhd->rbqhd", d_raw, key_window, preferred_element_type=jnp.float32
        )
        d_query = d_query + gathered_query.reshape(level_depth, window_span, HEADS, HEAD_DIM)
        d_keyw = jnp.einsum(
            "rbqhk,rbqhd->rbkhd", d_raw, query_blocks, preferred_element_type=jnp.float32
        )
        prob_low = (
            probs[level].astype(jnp.bfloat16).reshape(level_depth, count, query_len, HEADS, 3 * NR)
        )
        d_valuew = jnp.einsum(
            "rbqhk,rbqhd->rbkhd", prob_low, grad_blocks, preferred_element_type=jnp.float32
        )
        level_grads.append(
            jnp.concatenate(
                [
                    d_keyw.reshape(level_depth, count, 3 * NR, window_width),
                    d_valuew.reshape(level_depth, count, 3 * NR, window_width),
                ],
                axis=3,
            )
        )
    owned = []
    sends = []
    for level in range(near + 1):
        count = window_span // (NR * 2**level)
        folded = fold_windows(level_grads[level], count)
        owned.append(folded[:, NR : NR + count * NR])
        sends.append(jnp.concatenate([folded[:, :NR], folded[:, -NR:]], axis=1))
    returned_edges = [with_halo(item, (("seq", 1),), NR) for item in sends]
    arrived = [(item[:, :NR], item[:, -NR:]) for item in returned_edges]
    for level in range(near + 1):
        extent = owned[level].shape[1]
        from_left, from_right = arrived[level]
        owned[level] = (
            owned[level]
            + jnp.pad(from_left, ((0, 0), (0, extent - NR), (0, 0)))
            + jnp.pad(from_right, ((0, 0), (extent - NR, 0), (0, 0)))
        )
    far_parts = []
    for level in far_levels:
        block = NR * 2**level
        whole_count = length // 2**level
        corner = start // block * NR
        canvas = jnp.zeros((level_depth, whole_count + 2 * NR, 2 * window_width), jnp.float32)
        canvas = lax.dynamic_update_slice_in_dim(canvas, level_grads[level][:, 0], corner, axis=1)
        far_parts.append(
            canvas[:, NR : NR + whole_count].reshape(
                level_depth, seq_count, window_span // 2**level, 2 * window_width
            )
        )
    stacked = jnp.concatenate(far_parts, axis=2).reshape(
        level_depth, seq_count * far_total, 2 * window_width
    )
    returned = lax.psum_scatter(
        stacked.astype(jnp.bfloat16), "seq", scatter_dimension=1, tiled=True
    ).astype(jnp.float32)
    offset = 0
    for level in far_levels:
        local_count = window_span // 2**level
        owned.append(returned[:, offset : offset + local_count])
        offset += local_count
    carry = jnp.zeros_like(owned[top])
    for level in range(top, 0, -1):
        level_total = owned[level] + carry
        extent = level_total.shape[1]
        carry = jnp.broadcast_to(
            0.5 * level_total[:, :, None, :], (level_depth, extent, 2, 2 * window_width)
        ).reshape(level_depth, 2 * extent, 2 * window_width)
    level_zero = owned[0] + carry
    d_query_low = d_query.reshape(flat, window_width).astype(jnp.bfloat16)
    d_keys = level_zero[..., :window_width].reshape(flat, window_width).astype(jnp.bfloat16)
    d_values = level_zero[..., window_width:].reshape(flat, window_width).astype(jnp.bfloat16)
    query_grad = crossprod(first, d_query_low)
    querybias_grad = jnp.sum(d_query_low.astype(jnp.float32), axis=0)
    key_grad = crossprod(first, d_keys)
    value_grad = crossprod(first, d_values)
    valuebias_grad = jnp.sum(d_values.astype(jnp.float32), axis=0)
    first_cotangent = (
        backprod(d_query_low, query_proj)
        + backprod(d_keys, key_proj)
        + backprod(d_values, value_proj)
    )
    token_norm_gradient, prenorm_gain_gradient, prenorm_shift_gradient = first_pullback(
        first_cotangent.reshape(level_depth, window_span, window_width)
    )
    input_grad = (d_mid + token_norm_gradient).astype(jnp.bfloat16)
    summed = lax.psum(
        (
            prenorm_gain_gradient,
            prenorm_shift_gradient,
            query_grad,
            querybias_grad,
            key_grad,
            value_grad,
            valuebias_grad,
            output_grad,
            outputbias_grad,
            midgain_grad,
            midshift_grad,
            inner_grad,
            innerbias_grad,
            outer_grad,
            outerbias_grad,
        ),
        ("rows", "seq"),
    )
    return (
        layer_output,
        input_grad,
        summed[0],
        summed[1],
        summed[2],
        summed[3],
        summed[4],
        summed[5],
        summed[6],
        summed[7],
        summed[8],
        summed[9],
        summed[10],
        summed[11],
        summed[12],
        summed[13],
        summed[14],
    )


def solution(mesh):
    in_specs = (
        P("rows", "seq", None),
        P("rows", "seq"),
        P(),
        P(),
        P(),
        P(),
        P(),
        P(),
        P(),
        P(),
        P(),
        P(),
        P(),
        P(),
        P(),
        P(),
        P(),
        P("rows", "seq", None),
    )
    out_specs = (
        P("rows", "seq", None),
        P("rows", "seq", None),
        P(),
        P(),
        P(),
        P(),
        P(),
        P(),
        P(),
        P(),
        P(),
        P(),
        P(),
        P(),
        P(),
        P(),
        P(),
    )
    return jax.shard_map(shards, mesh=mesh, in_specs=in_specs, out_specs=out_specs, check_vma=False)
```

profile of v0, /device:TPU:0, one launch (start us, length us, event | category | flops | bytes accessed | tf_op | source)
XLA Modules:
  0.0 1113.7 jit_solution(16854671438747096323)
XLA Ops:
  17.9 5.5 collective-permute-start.8
  25.3 5.1 collective-permute-start.6
  31.1 2.9 collective-permute-start.4
  37.7 11.3 %all_gather.6 = bf16[1,1024]{1,0:T(2,128)(2,1)S(1)} all-gather(bf16[1,256]{1,0:T(2,128)(2,1)S(1)} %get-tuple-element.131), channel_id=1, replica_groups=mesh['rows'=8,'seq'=4] {'seq'}, dimensions={1}, use_global_device_ids=true | all-gather | bytes 2560 | tf_op jit(solution)/shard_map/all_gather | solution.py:153
  58.6 49.1 %gather_fusion = s32[12288]{0:T(1024)S(1)} fusion(s32[1024]{0:T(1024)S(1)} %bitcast.1032, s32[12288]{0:T(1024)S(1)} %broadcast_clamp_fusion.4), kind=kCustom, calls=%fused_computation | custom fusion | bytes 147456 | tf_op jit(solution)/shard_map/jit(_take)/gather | solution.py:82
  108.9 76.6 %gather_fusion.1 = s32[12288]{0:T(1024)S(1)} fusion(s32[512]{0:T(512)S(1)} %bitcast.1031, s32[12288]{0:T(1024)S(1)} %broadcast_clamp_fusion.3), kind=kCustom, calls=%fused_computation.1 | custom fusion | bytes 147456 | tf_op jit(solution)/shard_map/jit(_take)/gather | solution.py:82
  185.6 20.5 %fusion.298 = pred[256,48]{1,0:T(8,128)(4,1)S(1)} fusion(s32[]{:T(128)} %bitcast.88, s32[]{:T(128)} %bitcast.89, s32[]{:T(128)} %bitcast.90, s32[]{:T(128)} %bitcast.91, s32[]{:T(128)} %bitcast.92, s32[]{:T(128)} %bitcast.94, s32[]{:T(128)} %bitcast.93, s32[]{:T(128)} %bitcast.39, s32[]{:T(128)} %bitcast.41, s32[]{:T(128)} %bitcast.43, s32[]{:T(128)} %bitcast.45, ...), kind=kLoop, calls=%fused_computation.457 | loop fusion | flops 1253376 | bytes 15488 | tf_op jit(solution)/shard_map/and | solution.py:86
  206.2 73.0 %gather_fusion.4 = s32[12288]{0:T(1024)S(1)} fusion(s32[64]{0:T(128)S(1)} %fusion.396, s32[12288]{0:T(1024)S(1)} %broadcast_clamp_fusion), kind=kCustom, calls=%fused_computation.4 | custom fusion | bytes 147456 | tf_op jit(solution)/shard_map/jit(_take)/gather | solution.py:82
  280.0 73.0 %gather_fusion.3 = s32[12288]{0:T(1024)S(1)} fusion(s32[128]{0:T(128)S(1)} %fusion.395, s32[12288]{0:T(1024)S(1)} %broadcast_clamp_fusion.1), kind=kCustom, calls=%fused_computation.3 | custom fusion | bytes 147456 | tf_op jit(solution)/shard_map/jit(_take)/gather | solution.py:82
  353.9 76.2 %gather_fusion.2 = s32[12288]{0:T(1024)S(1)} fusion(s32[256]{0:T(256)S(1)} %bitcast.1030, s32[12288]{0:T(1024)S(1)} %broadcast_clamp_fusion.2), kind=kCustom, calls=%fused_computation.2 | custom fusion | bytes 147456 | tf_op jit(solution)/shard_map/jit(_take)/gather | solution.py:82
  432.5 14.1 %all-gather = bf16[1,32,1,1024]{3,1,2,0:T(8,128)(2,1)} all-gather(bf16[1,8,1,1024]{3,1,2,0:T(8,128)(2,1)S(1)} %fusion.350), channel_id=2, replica_groups=mesh['rows'=8,'seq'=4] {'seq'}, dimensions={1}, use_global_device_ids=true | all-gather | bytes 81920 | tf_op jit(solution)/shard_map/all_gather | solution.py:152
  469.2 4.5 collective-permute-start.2
  476.6 5.2 collective-permute-start
  493.3 2.7 fusion.457
  511.2 3.2 reshape.3209
  514.4 3.4 fusion.458
  572.9 11.7 %reshape.3208 = bf16[16,48,8,64]{3,2,1,0:T(8,128)(2,1)} reshape(bf16[1,16,48,512]{3,2,1,0:T(8,128)(2,1)} %get-tuple-element.74) | data formatting | bytes 1572864 | tf_op jit(solution)/shard_map/reshape.51
  591.9 2.6 reshape.3303
  615.7 3.0 fusion.80
  620.8 2.6 fusion.460
  650.5 2.8 fusion.99
  661.6 2.9 multiply_reduce_fusion.2
  671.4 2.6 convolution_bitcast_fusion.9
  678.0 3.8 multiply_reduce_fusion.1
  685.2 2.9 multiply_reduce_fusion
  736.8 2.7 copy.549
  739.4 3.7 reshape.3270
  743.1 4.5 copy.547
  747.7 3.7 reshape.3269
  756.6 2.9 fusion.132
  759.6 2.9 fusion.414
  764.1 3.0 copy.553
  767.1 2.7 reshape.3275
  778.4 5.2 collective-permute-start.18
  784.8 5.2 collective-permute-start.16
  792.9 5.2 collective-permute-start.14
  800.4 3.1 copy.551
  803.5 2.7 reshape.3274
  815.4 2.6 reshape.3299
  818.1 3.5 convert_reduce_fusion.5
  826.8 5.2 collective-permute-start.12
  835.0 5.3 collective-permute-start.10
  852.1 3.0 broadcast_in_dim.413
  865.5 2.6 reshape.3258
  868.1 2.5 copy.529
  879.5 2.6 fusion.123
  885.9 43.0 %all-reduce.24 = (f32[512]{0:T(512)}, f32[512]{0:T(512)}, f32[512]{0:T(512)}, f32[512]{0:T(512)}, f32[512]{0:T(512)}, /*index=5*/f32[512]{0:T(512)}, f32[512]{0:T(512)}, f32[2048]{0:T(1024)}, f32[512]{0:T(512)}) all-reduce(f32[512]{0:T(512)S(1)} %get-tuple-element.19, ...), channel_id=1, replica_groups=mesh['rows'=8,'seq'=4] {'rows','seq'}, use_global_device_ids=true, to_apply=%region_28.29 | all-reduce | flops 6144 | bytes 49152 | tf_op jit(solution)/shard_map/psum | solution.py:354
  931.0 164.4 %all-reduce.28.cloned.1.call-done = (f32[512,512]{1,0:T(8,128)}, f32[512,512]{1,0:T(8,128)}, f32[512,512]{1,0:T(8,128)}, f32[512,512]{1,0:T(8,128)}, f32[512,2048]{1,0:T(8,128)}, /*index=5*/f32[2048,512]{1,0:T(8,128)}) async-done(((f32[512,512]{1,0:T(8,128)}, f32[512,512]{1,0:T(8,128)}, f32[512,512]{1,0:T(8,128)}, f32[512,512]{1,0:T(8,128)}, f32[512,2048]{1,0:T(8,128)}, /*index=5*/f32[2048,512]{1,0:T(8,128)}), ...) | async-done | bytes 12582928 | tf_op jit(solution)/shard_map/psum | solution.py:354
  (813 shorter events, 352.9 us)
Async XLA Ops:
  7.2 617.3 %copy-start = (bf16[2048,512]{1,0:T(8,128)(2,1)S(1)}, bf16[2048,512]{1,0:T(8,128)(2,1)}, u32[]{:S(2)}) copy-start(bf16[2048,512]{1,0:T(8,128)(2,1)} %param.33) | copy-start | bytes 6291460
  7.2 817.4 %reduce-scatter.2.cloned.1.call-start = ((), (), s32[]{:S(2)}) async-start(), calls=%async_computation.1 | async-start | bytes 81920 | tf_op jit(solution)/shard_map/reduce_scatter | solution.py:321
  15.4 21.7 %copy-start.172 = (s32[1,256]{1,0:T(1,128)S(1)}, s32[1,256]{1,0:T(1,128)}, u32[]{:S(2)}) copy-start(s32[1,256]{1,0:T(1,128)} %param.19) | copy-start | bytes 3076
  15.9 33.1 %copy-start.53 = (bf16[1,64,1,1024]{3,1,2,0:T(8,128)(2,1)}, bf16[1,64,1,1024]{3,1,2,0:T(8,128)(2,1)S(1)}, u32[]{:S(2)}) copy-start(bf16[1,64,1,1024]{3,1,2,0:T(8,128)(2,1)S(1)} %get-tuple-element.58) | copy-start | bytes 393220
  16.3 39.8 %copy-start.73 = (bf16[256,512]{1,0:T(8,128)(2,1)S(1)}, bf16[256,512]{1,0:T(8,128)(2,1)}, u32[]{:S(2)}) copy-start(bf16[256,512]{1,0:T(8,128)(2,1)} %copy-done.72) | copy-start | bytes 786436
  16.3 39.8 %copy-start.75 = (bf16[256,512]{1,0:T(8,128)(2,1)S(1)}, bf16[256,512]{1,0:T(8,128)(2,1)}, u32[]{:S(2)}) copy-start(bf16[256,512]{1,0:T(8,128)(2,1)} %copy-done.74) | copy-start | bytes 786436
  16.4 36.4 %copy-start.70 = (bf16[1,32,1,1024]{3,1,2,0:T(8,128)(2,1)}, bf16[1,32,1,1024]{3,1,2,0:T(8,128)(2,1)S(1)}, u32[]{:S(2)}) copy-start(bf16[1,32,1,1024]{3,1,2,0:T(8,128)(2,1)S(1)} %get-tuple-element.60) | copy-start | bytes 196612
  17.9 465.4 %collective-permute-start.8 = (bf16[1,16,1024]{2,1,0:T(8,128)(2,1)}, bf16[1,16,1024]{2,1,0:T(8,128)(2,1)}, u32[]{:S(2)}, u32[]{:S(2)}) collective-permute-start(bf16[1,16,1024]{2,1,0:T(8,128)(2,1)} %bitcast.800.clone.2), channel_id=1, source_target_pairs={{0,1},{1,2},{2,3},{4,5},{5,6},{6,7},{8,9},{9,10},{10,11},{12,13},{... | collective-permute-start | bytes 98312 | tf_op jit(solution)/shard_map/ppermute | solution.py:23
  23.4 461.1 %collective-permute-start.9 = (bf16[1,16,1024]{2,1,0:T(8,128)(2,1)}, bf16[1,16,1024]{2,1,0:T(8,128)(2,1)}, u32[]{:S(2)}, u32[]{:S(2)}) collective-permute-start(bf16[1,16,1024]{2,1,0:T(8,128)(2,1)} %bitcast.800.clone.2), channel_id=1, source_target_pairs={{1,0},{2,1},{3,2},{5,4},{6,5},{7,6},{9,8},{10,9},{11,10},{13,12},{... | collective-permute-start | bytes 98312 | tf_op jit(solution)/shard_map/ppermute | solution.py:26
  25.3 450.0 %collective-permute-start.6 = (bf16[1,16,1024]{2,1,0:T(8,128)(2,1)}, bf16[1,16,1024]{2,1,0:T(8,128)(2,1)}, u32[]{:S(2)}, u32[]{:S(2)}) collective-permute-start(bf16[1,16,1024]{2,1,0:T(8,128)(2,1)} %get-tuple-element.122), channel_id=1, source_target_pairs={{0,1},{1,2},{2,3},{4,5},{5,6},{6,7},{8,9},{9,10},{10,11},{12,13},{... | collective-permute-start | bytes 98312 | tf_op jit(solution)/shard_map/ppermute | solution.py:23
  31.1 436.8 %collective-permute-start.4 = (bf16[1,16,1024]{2,1,0:T(8,128)(2,1)}, bf16[1,16,1024]{2,1,0:T(8,128)(2,1)}, u32[]{:S(2)}, u32[]{:S(2)}) collective-permute-start(bf16[1,16,1024]{2,1,0:T(8,128)(2,1)} %get-tuple-element.114), channel_id=1, source_target_pairs={{0,1},{1,2},{2,3},{4,5},{5,6},{6,7},{8,9},{9,10},{10,11},{12,13},{... | collective-permute-start | bytes 98312 | tf_op jit(solution)/shard_map/ppermute | solution.py:23
  34.0 435.2 %collective-permute-start.5 = (bf16[1,16,1024]{2,1,0:T(8,128)(2,1)}, bf16[1,16,1024]{2,1,0:T(8,128)(2,1)}, u32[]{:S(2)}, u32[]{:S(2)}) collective-permute-start(bf16[1,16,1024]{2,1,0:T(8,128)(2,1)} %get-tuple-element.115), channel_id=1, source_target_pairs={{1,0},{2,1},{3,2},{5,4},{6,5},{7,6},{9,8},{10,9},{11,10},{13,12},{... | collective-permute-start | bytes 98312 | tf_op jit(solution)/shard_map/ppermute | solution.py:26
  35.3 73.3 %copy-start.189 = (s32[256]{0:T(256)}, s32[256]{0:T(256)S(1)}, u32[]{:S(2)}) copy-start(s32[256]{0:T(256)S(1)} %get-tuple-element.204) | copy-start | bytes 3076
  206.2 246.2 %copy-start.93 = (pred[256,48]{0,1:T(8,128)(4,1)}, pred[256,48]{0,1:T(8,128)(4,1)S(1)}, u32[]{:S(2)}) copy-start(pred[256,48]{0,1:T(8,128)(4,1)S(1)} %copy.410) | copy-start | bytes 36868
  280.0 73.8 %copy-start.184 = (s32[256]{0:T(256)S(1)}, s32[256]{0:T(256)}, u32[]{:S(2)}) copy-start(s32[256]{0:T(256)} %copy-done.183) | copy-start | bytes 3076
  280.0 73.8 %copy-start.186 = (s32[256]{0:T(256)S(1)}, s32[256]{0:T(256)}, u32[]{:S(2)}) copy-start(s32[256]{0:T(256)} %copy-done.185) | copy-start | bytes 3076
  353.8 77.0 %copy-start.2 = (bf16[1,256,512]{2,1,0:T(8,128)(2,1)S(1)}, bf16[1,256,512]{2,1,0:T(8,128)(2,1)}, u32[]{:S(2)}) copy-start(bf16[1,256,512]{2,1,0:T(8,128)(2,1)} %param.18) | copy-start | bytes 786436
  353.8 77.0 %copy-start.155 = (f32[512]{0:T(512)S(1)}, f32[512]{0:T(512)}, u32[]{:S(2)}) copy-start(f32[512]{0:T(512)} %param.20) | copy-start | bytes 6148
  353.8 77.0 %copy-start.158 = (f32[256]{0:T(256)S(1)}, f32[256]{0:T(256)}, u32[]{:S(2)}) copy-start(f32[256]{0:T(256)} %copy-done.157) | copy-start | bytes 3076
  353.8 77.0 %copy-start.170 = (f32[256]{0:T(256)S(1)}, f32[256]{0:T(256)}, u32[]{:S(2)}) copy-start(f32[256]{0:T(256)} %copy-done.169) | copy-start | bytes 3076
  353.8 77.0 %copy-start.180 = (f32[512]{0:T(512)S(1)}, f32[512]{0:T(512)}, u32[]{:S(2)}) copy-start(f32[512]{0:T(512)} %param.21) | copy-start | bytes 6148
  353.8 77.0 %copy-start.198 = (f32[512]{0:T(512)S(1)}, f32[512]{0:T(512)}, u32[]{:S(2)}) copy-start(f32[512]{0:T(512)} %param.23) | copy-start | bytes 6148
  430.0 19.0 %copy-start.38 = (bf16[1,128,1,1024]{3,1,2,0:T(8,128)(2,1)S(1)}, bf16[1,128,1,1024]{3,1,2,0:T(8,128)(2,1)}, u32[]{:S(2)}) copy-start(bf16[1,128,1,1024]{3,1,2,0:T(8,128)(2,1)} %get-tuple-element.56) | copy-start | bytes 786436
  430.1 20.8 %copy-start.91 = (s32[16,16,48]{2,1,0:T(8,128)S(1)}, s32[16,16,48]{2,1,0:T(8,128)}, u32[]{:S(2)}) copy-start(s32[16,16,48]{2,1,0:T(8,128)} %gather.37) | copy-start | bytes 147460
  432.4 29.3 %copy-start.13 = (bf16[256,512]{0,1:T(8,128)(2,1)}, bf16[256,512]{0,1:T(8,128)(2,1)S(1)}, u32[]{:S(2)}) copy-start(bf16[256,512]{0,1:T(8,128)(2,1)S(1)} %copy.401) | copy-start | bytes 786436
  453.3 21.2 %copy-start.103 = (f32[256,8]{0,1:T(8,128)}, f32[256,8]{0,1:T(8,128)S(1)}, u32[]{:S(2)}) copy-start(f32[256,8]{0,1:T(8,128)S(1)} %get-tuple-element.164) | copy-start | bytes 24580
  453.3 20.4 %copy-start.54 = (bf16[1,64,1,1024]{3,1,2,0:T(8,128)(2,1)S(1)}, bf16[1,64,1,1024]{3,1,2,0:T(8,128)(2,1)}, u32[]{:S(2)}) copy-start(bf16[1,64,1,1024]{3,1,2,0:T(8,128)(2,1)} %copy-done.53) | copy-start | bytes 393220
  460.6 21.2 %copy-start.71 = (bf16[1,32,1,1024]{3,1,2,0:T(8,128)(2,1)S(1)}, bf16[1,32,1,1024]{3,1,2,0:T(8,128)(2,1)}, u32[]{:S(2)}) copy-start(bf16[1,32,1,1024]{3,1,2,0:T(8,128)(2,1)} %copy-done.70) | copy-start | bytes 196612
  467.9 8.7 collective-permute-start.7
  469.2 18.6 %collective-permute-start.2 = (bf16[1,16,1024]{2,1,0:T(8,128)(2,1)}, bf16[1,16,1024]{2,1,0:T(8,128)(2,1)S(1)}, u32[]{:S(2)}, u32[]{:S(2)}) collective-permute-start(bf16[1,16,1024]{2,1,0:T(8,128)(2,1)} %get-tuple-element.101), channel_id=1, source_target_pairs={{0,1},{1,2},{2,3},{4,5},{5,6},{6,7},{8,9},{9,10},{10,11},{12,13},{... | collective-permute-start | bytes 98312 | tf_op jit(solution)/shard_map/ppermute | solution.py:23
  475.3 12.5 %collective-permute-start.3 = (bf16[1,16,1024]{2,1,0:T(8,128)(2,1)}, bf16[1,16,1024]{2,1,0:T(8,128)(2,1)S(1)}, u32[]{:S(2)}, u32[]{:S(2)}) collective-permute-start(bf16[1,16,1024]{2,1,0:T(8,128)(2,1)} %get-tuple-element.102), channel_id=1, source_target_pairs={{1,0},{2,1},{3,2},{5,4},{6,5},{7,6},{9,8},{10,9},{11,10},{13,12},{... | collective-permute-start | bytes 98312 | tf_op jit(solution)/shard_map/ppermute | solution.py:26
  476.6 30.7 %collective-permute-start = (bf16[1,16,1024]{2,1,0:T(8,128)(2,1)}, bf16[1,16,1024]{2,1,0:T(8,128)(2,1)}, u32[]{:S(2)}, u32[]{:S(2)}) collective-permute-start(bf16[1,16,1024]{2,1,0:T(8,128)(2,1)} %get-tuple-element.85), channel_id=1, source_target_pairs={{0,1},{1,2},{2,3},{4,5},{5,6},{6,7},{8,9},{9,10},{10,11},{12,13},{... | collective-permute-start | bytes 98312 | tf_op jit(solution)/shard_map/ppermute | solution.py:23
  483.2 24.1 %collective-permute-start.1 = (bf16[1,16,1024]{2,1,0:T(8,128)(2,1)}, bf16[1,16,1024]{2,1,0:T(8,128)(2,1)}, u32[]{:S(2)}, u32[]{:S(2)}) collective-permute-start(bf16[1,16,1024]{2,1,0:T(8,128)(2,1)} %get-tuple-element.86), channel_id=1, source_target_pairs={{1,0},{2,1},{3,2},{5,4},{6,5},{7,6},{9,8},{10,9},{11,10},{13,12},{... | collective-permute-start | bytes 98312 | tf_op jit(solution)/shard_map/ppermute | solution.py:26
  524.0 19.1 %copy-start.84 = (pred[16,16,48]{2,1,0:T(8,128)(4,1)S(1)}, pred[16,16,48]{2,1,0:T(8,128)(4,1)}, u32[]{:S(2)}) copy-start(pred[16,16,48]{2,1,0:T(8,128)(4,1)} %fusion.304) | copy-start | bytes 36868
  569.0 16.4 %copy-start.96 = (pred[256,48]{0,1:T(8,128)(4,1)S(1)}, pred[256,48]{0,1:T(8,128)(4,1)}, u32[]{:S(2)}) copy-start(pred[256,48]{0,1:T(8,128)(4,1)} %copy.406) | copy-start | bytes 36868
  598.0 80.1 %copy-start.61 = (f32[16,16,8]{1,2,0:T(8,128)}, f32[16,16,8]{1,2,0:T(8,128)S(1)}, u32[]{:S(2)}) copy-start(f32[16,16,8]{1,2,0:T(8,128)S(1)} %fusion.344) | copy-start | bytes 24580
  775.9 319.5 %all-reduce.28.cloned.1.call-start = ((), (), s32[]{:S(2)}) async-start(), calls=%async_computation.2 | async-start | bytes 25165824 | tf_op jit(solution)/shard_map/psum | solution.py:354
  778.4 47.1 %collective-permute-start.18 = (f32[1,16,1024]{2,1,0:T(8,128)}, f32[1,16,1024]{2,1,0:T(8,128)}, u32[]{:S(2)}, u32[]{:S(2)}) collective-permute-start(f32[1,16,1024]{2,1,0:T(8,128)} %get-tuple-element.105), channel_id=1, source_target_pairs={{0,1},{1,2},{2,3},{4,5},{5,6},{6,7},{8,9},{9,10},{10,11},{12,13},{... | collective-permute-start | bytes 196616 | tf_op jit(solution)/shard_map/ppermute | solution.py:23
  783.5 43.2 %collective-permute-start.19 = (f32[1,16,1024]{2,1,0:T(8,128)}, f32[1,16,1024]{2,1,0:T(8,128)}, u32[]{:S(2)}, u32[]{:S(2)}) collective-permute-start(f32[1,16,1024]{2,1,0:T(8,128)} %get-tuple-element.106), channel_id=1, source_target_pairs={{1,0},{2,1},{3,2},{5,4},{6,5},{7,6},{9,8},{10,9},{11,10},{13,12},{... | collective-permute-start | bytes 196616 | tf_op jit(solution)/shard_map/ppermute | solution.py:26
  784.8 48.9 %collective-permute-start.16 = (f32[1,16,1024]{2,1,0:T(8,128)}, f32[1,16,1024]{2,1,0:T(8,128)}, u32[]{:S(2)}, u32[]{:S(2)}) collective-permute-start(f32[1,16,1024]{2,1,0:T(8,128)} %get-tuple-element.91), channel_id=1, source_target_pairs={{0,1},{1,2},{2,3},{4,5},{5,6},{6,7},{8,9},{9,10},{10,11},{12,13},{... | collective-permute-start | bytes 196616 | tf_op jit(solution)/shard_map/ppermute | solution.py:23
  790.0 45.0 %collective-permute-start.17 = (f32[1,16,1024]{2,1,0:T(8,128)}, f32[1,16,1024]{2,1,0:T(8,128)}, u32[]{:S(2)}, u32[]{:S(2)}) collective-permute-start(f32[1,16,1024]{2,1,0:T(8,128)} %get-tuple-element.92), channel_id=1, source_target_pairs={{1,0},{2,1},{3,2},{5,4},{6,5},{7,6},{9,8},{10,9},{11,10},{13,12},{... | collective-permute-start | bytes 196616 | tf_op jit(solution)/shard_map/ppermute | solution.py:26
  792.9 51.1 %collective-permute-start.14 = (f32[1,16,1024]{2,1,0:T(8,128)}, f32[1,16,1024]{2,1,0:T(8,128)}, u32[]{:S(2)}, u32[]{:S(2)}) collective-permute-start(f32[1,16,1024]{2,1,0:T(8,128)} %get-tuple-element.76), channel_id=1, source_target_pairs={{0,1},{1,2},{2,3},{4,5},{5,6},{6,7},{8,9},{9,10},{10,11},{12,13},{... | collective-permute-start | bytes 196616 | tf_op jit(solution)/shard_map/ppermute | solution.py:23
  825.5 19.8 %collective-permute-start.15 = (f32[1,16,1024]{2,1,0:T(8,128)}, f32[1,16,1024]{2,1,0:T(8,128)}, u32[]{:S(2)}, u32[]{:S(2)}) collective-permute-start(f32[1,16,1024]{2,1,0:T(8,128)} %get-tuple-element.77), channel_id=1, source_target_pairs={{1,0},{2,1},{3,2},{5,4},{6,5},{7,6},{9,8},{10,9},{11,10},{13,12},{... | collective-permute-start | bytes 196616 | tf_op jit(solution)/shard_map/ppermute | solution.py:26
  826.8 22.9 %collective-permute-start.12 = (f32[1,16,1024]{2,1,0:T(8,128)}, f32[1,16,1024]{2,1,0:T(8,128)}, u32[]{:S(2)}, u32[]{:S(2)}) collective-permute-start(f32[1,16,1024]{2,1,0:T(8,128)} %get-tuple-element.69), channel_id=1, source_target_pairs={{0,1},{1,2},{2,3},{4,5},{5,6},{6,7},{8,9},{9,10},{10,11},{12,13},{... | collective-permute-start | bytes 196616 | tf_op jit(solution)/shard_map/ppermute | solution.py:23
  833.7 16.0 %collective-permute-start.13 = (f32[1,16,1024]{2,1,0:T(8,128)}, f32[1,16,1024]{2,1,0:T(8,128)}, u32[]{:S(2)}, u32[]{:S(2)}) collective-permute-start(f32[1,16,1024]{2,1,0:T(8,128)} %get-tuple-element.70), channel_id=1, source_target_pairs={{1,0},{2,1},{3,2},{5,4},{6,5},{7,6},{9,8},{10,9},{11,10},{13,12},{... | collective-permute-start | bytes 196616 | tf_op jit(solution)/shard_map/ppermute | solution.py:26
  835.0 20.1 %collective-permute-start.10 = (f32[1,16,1024]{2,1,0:T(8,128)}, f32[1,16,1024]{2,1,0:T(8,128)}, u32[]{:S(2)}, u32[]{:S(2)}) collective-permute-start(f32[1,16,1024]{2,1,0:T(8,128)} %get-tuple-element.64), channel_id=1, source_target_pairs={{0,1},{1,2},{2,3},{4,5},{5,6},{6,7},{8,9},{9,10},{10,11},{12,13},{... | collective-permute-start | bytes 196616 | tf_op jit(solution)/shard_map/ppermute | solution.py:23
  844.0 11.1 %collective-permute-start.11 = (f32[1,16,1024]{2,1,0:T(8,128)}, f32[1,16,1024]{2,1,0:T(8,128)}, u32[]{:S(2)}, u32[]{:S(2)}) collective-permute-start(f32[1,16,1024]{2,1,0:T(8,128)} %get-tuple-element.65), channel_id=1, source_target_pairs={{1,0},{2,1},{3,2},{5,4},{6,5},{7,6},{9,8},{10,9},{11,10},{13,12},{... | collective-permute-start | bytes 196616 | tf_op jit(solution)/shard_map/ppermute | solution.py:26
  885.0 43.9 %copy-start.188 = (f32[256]{0:T(256)S(1)}, f32[256]{0:T(256)}, u32[]{:S(2)}) copy-start(f32[256]{0:T(256)} %copy-done.187) | copy-start | bytes 3076
  (174 other events, 711.3 us)
Sparse Core Ops, SparseCore 0:
  776.0 19.7 reduce-scatter.1
  859.8 235.5 all-reduce.27
where the time goes:
time: 1130 us; the launch traced here: 1110 us
  local copies, waits for them, and re-layouts  620 us (55%)
  waiting for transfers between devices  164 us (15%)
  matrix products  100 us (9%)
  other arithmetic  80.5 us (7%)
  blocking collectives  68.3 us (6%)
  starting transfers between devices  62.2 us (6%)
  between operations  17.2 us (2%)
    gather x12, local copies, waits for them, and re-layouts, level_mask(): jnp.take(coarse_ids, jnp.clip(key_index, 0, coarse_count - 1), axis=1)  352 us
    psum x1, waiting for transfers between devices, shards(): lax.psum((prenorm_gain_gradient, prenorm_shift_gradient, query_grad, quer...  164 us
    ppermute x10, starting transfers between devices, with_halo(): lax.ppermute(lax.slice_in_dim(block, block.shape[dim] - width, None, axis...  49.3 us
    psum x1, blocking collectives, shards(): lax.psum((prenorm_gain_gradient, prenorm_shift_gradient, query_grad, quer...  43 us
    another operation x20, local copies, waits for them, and re-layouts  40.9 us
    unnamed x413, local copies, waits for them, and re-layouts  29.3 us
    and x5, other arithmetic, level_mask(): mask = mask & (key_ids != 0) & distant[None]  25.6 us
    reshape x10, local copies, waits for them, and re-layouts, shards(): gathered_query.reshape(level_depth, window_span, HEADS, HEAD_DIM)  23.3 us
  transfers between devices with their start and end apart: 22, of which 1 were waited for; matrix products, arithmetic and copies ran while one was open for 45% of the time, Pallas kernels for 0%

commit v1 on v0

v1 whole, which is shorter than its diff:
```python
import functools
import math

import jax
import jax.numpy as jnp
from jax import lax
from jax.experimental import pallas as pl
from jax.experimental.pallas import tpu as pltpu
from jax.sharding import PartitionSpec as P

HEADS = 8
HEAD_DIM = 64
NR = 16
LANES = 128
LOG_TWO = math.log(2.0)
EPSILON = 1e-05
MASKED = -1e30
F32 = jnp.float32
BF16 = jnp.bfloat16
MESH = pl.DeviceIdType.MESH

VEC_ROWS = 16
V_PREG, V_PRES, V_QB, V_VB, V_OB, V_MIDG, V_MIDS, V_OUTB, V_INNB = 0, 1, 2, 3, 4, 5, 6, 7, 8


def dot(a, b):
    return jnp.dot(a, b, preferred_element_type=F32)


def dot_nt(a, b):
    return lax.dot_general(a, b, (((1,), (1,)), ((), ())), preferred_element_type=F32)


def dot_tn(a, b):
    return lax.dot_general(a, b, (((0,), (0,)), ((), ())), preferred_element_type=F32)


def iota(shape, dim):
    return lax.broadcasted_iota(jnp.int32, shape, dim)


def mean(x):
    return jnp.mean(x, axis=-1, keepdims=True)


def total(x):
    return jnp.sum(x, axis=0, keepdims=True)


class Plan:
    def __init__(self, rows, seq, span, width, hidden):
        self.rows, self.seq, self.span, self.width, self.hidden = rows, seq, span, width, hidden
        self.near = (span // NR).bit_length() - 1
        self.length = span * seq
        self.top = (self.length // NR).bit_length() - 2
        self.chunk = 128
        self.chunks = span // self.chunk
        self.far = list(range(self.near + 1, self.top + 1))
        self.level_row = [0]
        at = 0
        for level in range(1, self.near + 1):
            self.level_row.append(at)
            at += span >> level
        self.far_row = at
        for level in self.far:
            self.level_row.append(at)
            at += span >> level
        self.coarse_rows = self.far_row + NR
        self.id_row = NR - 2
        self.slot, self.slot_len = [], []
        at = 0
        for level in range(self.top + 1):
            n = 2 * NR + max(self.chunk >> level, NR)
            self.slot.append(at)
            self.slot_len.append(n)
            at += n
        self.used = at
        self.slots = -(-at // LANES) * LANES
        self.far_slot = self.slot[self.near + 1]
        self.far_slots = self.slots - self.far_slot
        self.edge = NR * (self.near + 1)
        self.grad_rows = 4 * width + 2 * hidden
        ffn = hidden
        self.parts = [(0, ffn), (ffn, ffn + width), (2 * ffn + width, 3 * width)]
        self.counts = [2, 2, rows // 4, seq]
        self.swap = rows // 4 == 2
        self.scatter = []
        for off, n in self.parts:
            per = n // (2 * 2 * (rows // 4))
            self.scatter.append(per % (NR * seq) == 0)


def sequence(*steps):
    for step in steps:
        step()


def layer_kernel(
    plan,
    tok_hbm, ids_ref, vec_ref, inb_ref, wq_hbm, wk_hbm, wv_hbm, wo_hbm, w1_hbm, w2_hbm, up_hbm,
    out_ref, gin_ref, red_ref, vout_ref,
    tok, up, wq, wk, wv, wo, w1, w2, n1, n2, mid, racc, dsec, first, second, qh, att, dah, dq,
    level, edge, halo, farg, slots, levs, bias, probs, dslots, own, hsend, hrecv, fsend, frecv,
    coarse, dkv, grads, recv0, recv1, recv2, recv3, vstage, vrecv0, vrecv1, vrecv2, vrecv3, stats,
    in_sem, halo_send, halo_recv, far_send, far_recv, back_send, back_recv, fback_send, fback_recv,
    rs_send, rs_recv, ag_send, ag_recv, vec_send, vec_recv,
):
    span, width, hidden = plan.span, plan.width, plan.hidden
    seq, near, top = plan.seq, plan.near, plan.top
    tile = hidden // w1.shape[0]
    tiles = w1.shape[0]
    pairs = width // LANES
    blocks = 2 * pairs
    row_id, seq_id = lax.axis_index("rows"), lax.axis_index("seq")
    start = seq_id * span

    core = row_id % 2
    if plan.swap:
        stride_a, stride_b = 2 + 2 * core, 4 - 2 * core
    else:
        stride_a, stride_b = 2, 4
    count = plan.counts
    index = [
        core,
        (row_id // stride_a) % count[1],
        (row_id // stride_b) % count[2],
        seq_id,
    ]

    def peer(digit, k):
        other = (index[digit] + k) % count[digit]
        if digit == 3:
            return other, (row_id, other)
        stride = [1, stride_a, stride_b][digit]
        return other, (row_id + (other - index[digit]) * stride, seq_id)

    def remote(src, dst, send, recv, device):
        return pltpu.make_async_remote_copy(
            src_ref=src, dst_ref=dst, send_sem=send, recv_sem=recv,
            device_id=device, device_id_type=MESH,
        )

    loads = []

    def load(src, dst):
        copy = pltpu.make_async_copy(src, dst, in_sem.at[len(loads)])
        copy.start()
        loads.append(copy)
        return copy

    load_tok = load(tok_hbm.at[0], tok)
    load_q = load(wq_hbm, wq)
    load_k = load(wk_hbm, wk)
    load_v = load(wv_hbm, wv)
    load_up = load(up_hbm.at[0], up)
    load_o = load(wo_hbm, wo)
    load_1 = [load(w1_hbm.at[:, t * tile : (t + 1) * tile], w1.at[t]) for t in range(tiles)]
    load_2 = load(w2_hbm, w2)

    halo[...] = jnp.zeros_like(halo)
    hrecv[...] = jnp.zeros_like(hrecv)
    vstage[0] = jnp.zeros((VEC_ROWS, width), F32)

    barrier = pltpu.get_barrier_semaphore()
    greeted = 0
    for digit in range(4):
        for k in range(1, count[digit]):
            _, device = peer(digit, k)
            pl.semaphore_signal(barrier, inc=1, device_id=device, device_id_type=MESH)
            greeted += 1

    def vec(row):
        return vec_ref[row : row + 1, :]

    load_tok.wait()
    x = tok[...].astype(F32)
    center = x - mean(x)
    rstd = lax.rsqrt(mean(center * center) + EPSILON)
    normed = center * rstd
    n1[...] = normed
    stats[0] = jnp.broadcast_to(rstd, (span, LANES))
    first[...] = (normed * vec(0) + vec(1)).astype(BF16)
    load_k.wait()
    keys = dot(first[...], wk[...]).astype(BF16)
    load_v.wait()
    values = (dot(first[...], wv[...]) + vec(3)).astype(BF16)
    for b in range(pairs):
        level[b, :span] = keys[:, b * LANES : (b + 1) * LANES]
        level[pairs + b, :span] = values[:, b * LANES : (b + 1) * LANES]

    def averaging(rows_dim):
        shape = (plan.coarse_rows, span) if rows_dim == 0 else (span, plan.coarse_rows)
        r, p = iota(shape, rows_dim), iota(shape, 1 - rows_dim)
        matrix = jnp.zeros(shape, F32)
        for lv in range(1, top + 1):
            at = plan.level_row[lv]
            hit = (r - at == (p >> lv)) & (r >= at) & (r < at + (span >> lv))
            matrix = jnp.where(hit, 0.5**lv, matrix)
        return matrix.astype(BF16)

    matrix = averaging(0)
    ids_f = ids_ref[...].astype(F32)
    ids_wide = jnp.concatenate([ids_f, jnp.zeros((1, 2 * width - span), F32)], axis=1)
    far_at = plan.far_row
    for half, kv in enumerate((keys, values)):
        mixed = dot(matrix, kv)
        for b in range(pairs):
            level[half * pairs + b, span : span + far_at] = mixed[
                :far_at, b * LANES : (b + 1) * LANES
            ].astype(BF16)
        ids_half = jnp.broadcast_to(ids_wide[:, half * width : (half + 1) * width], (NR, width))
        farg[seq_id, :, half * width : (half + 1) * width] = jnp.where(
            iota((NR, width), 0) == plan.id_row, ids_half, mixed[far_at:]
        ).astype(BF16)

    def level_start(lv):
        return 0 if lv == 0 else span + plan.level_row[lv]

    for lv in range(near + 1):
        at, n = level_start(lv), span >> lv
        edge[0, :, lv * NR : (lv + 1) * NR] = level[:, at : at + NR]
        edge[1, :, lv * NR : (lv + 1) * NR] = level[:, at + n - NR : at + n]

    pl.semaphore_wait(barrier, greeted)

    def far_copy(k):
        _, device = peer(3, k)
        return remote(
            farg.at[seq_id], farg.at[seq_id], far_send.at[k - 1], far_recv.at[k - 1], device
        )

    def halo_copy(src, dst, send, recv, side):
        step = 2 * side - 1
        return remote(
            src.at[side], dst.at[1 - side], send.at[side], recv.at[1 - side],
            (row_id, seq_id + step),
        )

    def halo_start(src, dst, send, recv):
        @pl.when(seq_id > 0)
        def _():
            halo_copy(src, dst, send, recv, 0).start()

        @pl.when(seq_id < seq - 1)
        def _():
            halo_copy(src, dst, send, recv, 1).start()

    def halo_wait(src, dst, send, recv):
        @pl.when(seq_id > 0)
        def _():
            remote(
                src.at[0], dst.at[0], send.at[0], recv.at[0], (row_id, seq_id - 1)
            ).wait()

        @pl.when(seq_id < seq - 1)
        def _():
            remote(
                src.at[1], dst.at[1], send.at[1], recv.at[1], (row_id, seq_id + 1)
            ).wait()

    halo_start(edge, halo, halo_send, halo_recv)
    for k in range(1, seq):
        far_copy(k).start()

    load_q.wait()
    query = ((dot(first[...], wq[...]) + vec(2)).astype(BF16) * (1.0 / math.sqrt(HEAD_DIM))).astype(
        BF16
    )
    for b in range(pairs):
        qh[b] = query[:, b * LANES : (b + 1) * LANES]

    def slot_pieces(c):
        pieces = []
        for lv in range(near + 1):
            at, n = level_start(lv), span >> lv
            per = plan.chunk >> lv
            s0 = plan.slot[lv]
            if per >= NR:
                low, high = c * per - NR, c * per + per + NR
            else:
                low, high = -NR, n + NR
            if low < 0:
                pieces.append((s0, "low", lv * NR, NR))
                s0, low = s0 + NR, 0
            inner = min(high, n)
            pieces.append((s0, "own", at + low, inner - low))
            s0 += inner - low
            if high > n:
                pieces.append((s0, "high", lv * NR, NR))
        return pieces

    halo_wait(edge, halo, halo_send, halo_recv)
    for c in range(plan.chunks):
        for s0, kind, at, n in slot_pieces(c):
            if kind == "own":
                slots[c, :, s0 : s0 + n] = level[:, at : at + n]
            else:
                slots[c, :, s0 : s0 + n] = halo[0 if kind == "low" else 1, :, at : at + n]
    for k in range(1, seq):
        far_copy(k).wait()

    def far_select():
        pieces = []
        for lv in plan.far:
            per_log = (span >> lv).bit_length() - 1
            first_row = plan.level_row[lv] - plan.far_row
            j = (start // (NR << lv) - 1) * NR + iota((3 * NR, seq * NR), 0)
            column = (j >> per_log) * NR + (j & ((1 << per_log) - 1)) + first_row
            pieces.append((column == iota((3 * NR, seq * NR), 1)).astype(F32))
        rest = plan.far_slots - 3 * NR * len(plan.far)
        if rest:
            pieces.append(jnp.zeros((rest, seq * NR), F32))
        return jnp.concatenate(pieces, axis=0).astype(BF16)

    select = far_select()
    far_values = dot(select, farg[...].reshape(seq * NR, 2 * width)).astype(BF16)
    for c in range(plan.chunks):
        for b in range(blocks):
            slots[c, b, plan.far_slot :] = far_values[:, b * LANES : (b + 1) * LANES]

    row_ids = [farg[s].astype(F32)[plan.id_row : plan.id_row + 1, :span] for s in range(seq)]
    current = jnp.concatenate(row_ids, axis=1)
    level_ids = [current]
    for lv in range(1, top + 1):
        shifted = pltpu.roll(current, plan.length - (1 << (lv - 1)), 1)
        current = jnp.where(current == shifted, current, 0.0)
        level_ids.append(current)
    level_ids += [jnp.zeros_like(current)] * (8 - len(level_ids))
    stacked = jnp.concatenate(level_ids, axis=0).astype(BF16)
    for s in range(seq):
        levs[s] = stacked[:, s * span : (s + 1) * span]

    ids_rows = jnp.broadcast_to(ids_f, (8, span)).astype(BF16)
    slot_at = iota((1, plan.slots), 1)
    slot_level = jnp.zeros((1, plan.slots), jnp.int32)
    for lv in range(1, top + 1):
        slot_level = slot_level + (slot_at >= plan.slot[lv]).astype(jnp.int32)
    for c in range(plan.chunks):
        origin = start + c * plan.chunk
        j = slot_at
        for lv in range(top + 1):
            if (plan.chunk >> lv) >= NR:
                base = origin // (1 << lv) - NR
            else:
                base = (origin // (NR << lv) - 1) * NR
            here = slot_at - plan.slot[lv] + base
            j = here if lv == 0 else jnp.where(slot_level == lv, here, j)
        j = jnp.where(slot_at < plan.used, j, -1)
        goal = j << slot_level

        def gather_ids(s, found):
            hot = iota((span, plan.slots), 0) + s * span == goal
            return found + dot(levs[s], hot.astype(F32).astype(BF16))

        found = lax.fori_loop(0, seq, gather_ids, jnp.zeros((8, plan.slots), F32))
        own_level = iota((8, plan.slots), 0) == slot_level
        key_id = jnp.sum(jnp.where(own_level, found, 0.0), axis=0, keepdims=True)
        mine = (iota((plan.chunk, span), 1) == iota((plan.chunk, span), 0) + c * plan.chunk)
        query_id = dot_nt(mine.astype(F32).astype(BF16), ids_rows)[:, :1]
        inside = (goal >= 0) & (goal < plan.length) & (j >= 0)
        usable = inside & ((slot_level == 0) | (key_id > 0.5))
        key_id = jnp.where(usable, key_id, -1.0)
        position = origin + iota((plan.chunk, plan.slots), 0)
        off_block = (j >> 4) - (position >> (slot_level + 4))
        off_half = (j >> 3) - (position >> (slot_level + 3))
        reach = jnp.where(slot_level == 0, -1, 1)
        counted = (key_id == query_id) & (jnp.abs(off_block) <= 1) & (jnp.abs(off_half) > reach)
        bias[c] = jnp.where(counted, slot_level.astype(F32) * LOG_TWO, MASKED)

    lane = iota((1, LANES), 1)
    low_half = (lane < HEAD_DIM).astype(F32).astype(BF16)
    high_half = (lane >= HEAD_DIM).astype(F32).astype(BF16)
    low_lanes = iota((plan.chunk, LANES), 1) < HEAD_DIM

    def two_heads(block):
        return jnp.concatenate([block * low_half, block * high_half], axis=0)

    def merge_heads(both):
        return jnp.where(low_lanes, both[: plan.chunk], both[plan.chunk :])

    def chunk_rows(c):
        return pl.ds(pl.multiple_of(c * plan.chunk, plan.chunk), plan.chunk)

    def pair_lanes(b):
        return pl.ds(pl.multiple_of(b * LANES, LANES), LANES)

    def attend(i, carry):
        c, b = i // pairs, i % pairs
        q2 = two_heads(qh[b, chunk_rows(c)])
        offset = bias[c]
        score = dot_nt(q2, slots[c, b]) + jnp.concatenate([offset, offset], axis=0)
        peak = jnp.max(score, axis=1, keepdims=True)
        raised = jnp.exp(score - peak)
        prob = raised * (1.0 / jnp.sum(raised, axis=1, keepdims=True))
        low = prob.astype(BF16)
        probs[i] = low
        att[chunk_rows(c), pair_lanes(b)] = merge_heads(dot(low, slots[c, pairs + b])).astype(BF16)
        return carry

    lax.fori_loop(0, plan.chunks * pairs, attend, 0)

    received = [recv0, recv1, recv2, recv3]
    starts = [recv0.shape[1], recv1.shape[1], recv2.shape[1], recv3.shape[1]]
    step_of_part = []

    def region(part, digits):
        off, n = plan.parts[part]
        base = off
        for digit in range(digits):
            n = n // count[digit]
            base = base + index[digit] * n
        return base, n

    def rows_at(base, n):
        return pl.ds(pl.multiple_of(base, NR), n)

    def received_rows(part, digit, n):
        off, whole = plan.parts[part]
        share = whole // n
        return pl.ds(off // share, n)

    def rs_copy(part, digit, k):
        base, n = region(part, digit)
        other, device = peer(digit, k)
        if digit == 3 and not plan.scatter[part]:
            return remote(
                grads.at[rows_at(base, n)],
                received[digit].at[k - 1, received_rows(part, digit, n)],
                rs_send.at[part, digit, k - 1], rs_recv.at[part, digit, k - 1], device,
            )
        n = n // count[digit]
        return remote(
            grads.at[rows_at(base + other * n, n)],
            received[digit].at[k - 1, received_rows(part, digit, n)],
            rs_send.at[part, digit, k - 1], rs_recv.at[part, digit, k - 1], device,
        )

    def rs_start(part, digit):
        for k in range(1, count[digit]):
            rs_copy(part, digit, k).start()

    def rs_finish(part, digit):
        for k in range(1, count[digit]):
            rs_copy(part, digit, k).wait_recv()
        gather_all = digit == 3 and not plan.scatter[part]
        base, n = region(part, digit if gather_all else digit + 1)
        off, whole = plan.parts[part]
        at = off // (whole // n)
        target = red_ref if digit == 3 else grads
        block = 64 if n % 64 == 0 else NR

        def add(i, carry):
            here = rows_at(base + i * block, block)
            there = pl.ds(pl.multiple_of(at + i * block, NR), block)
            if gather_all:
                acc = jnp.zeros((block, width), F32)
                for s in range(seq):
                    slot = (seq_id - s + seq - 1) % seq
                    theirs = received[digit][jnp.minimum(slot, seq - 2), there].astype(F32)
                    acc = acc + jnp.where(seq_id == s, grads[here].astype(F32), theirs)
            else:
                acc = grads[here].astype(F32)
                for k in range(1, count[digit]):
                    acc = acc + received[digit][k - 1, there].astype(F32)
            target[here] = acc.astype(BF16)
            return carry

        lax.fori_loop(0, n // block, add, 0)

    def ag_copy(part, digit, k):
        base, n = region(part, digit + 1)
        _, device = peer(digit, k)
        return remote(
            red_ref.at[rows_at(base, n)], red_ref.at[rows_at(base, n)],
            ag_send.at[part, digit, k - 1], ag_recv.at[part, digit, k - 1], device,
        )

    def ag_start(part, digit):
        if digit == 3 and not plan.scatter[part]:
            return
        for k in range(1, count[digit]):
            ag_copy(part, digit, k).start()

    def ag_finish(part, digit):
        if digit == 3 and not plan.scatter[part]:
            return
        for k in range(1, count[digit]):
            ag_copy(part, digit, k).wait_recv()

    def part_steps(part):
        steps = [lambda: rs_start(part, 0)]
        for digit in range(1, 4):
            steps.append(
                functools.partial(
                    sequence,
                    functools.partial(rs_finish, part, digit - 1),
                    functools.partial(rs_start, part, digit),
                )
            )
        steps.append(
            functools.partial(
                sequence, functools.partial(rs_finish, part, 3), functools.partial(ag_start, part, 3)
            )
        )
        for digit in (2, 1, 0):
            steps.append(
                functools.partial(
                    sequence,
                    functools.partial(ag_finish, part, digit + 1),
                    functools.partial(ag_start, part, digit),
                )
            )
        steps.append(functools.partial(ag_finish, part, 0))
        return steps

    part_a, part_b, part_c = (part_steps(part) for part in range(3))

    load_o.wait()
    load_up.wait()
    res = tok[...].astype(F32) + dot(att[...], wo[...]) + vec(4)
    mid[...] = res
    center = res - mean(res)
    rstd = lax.rsqrt(mean(center * center) + EPSILON)
    normed = center * rstd
    n2[...] = normed
    stats[1] = jnp.broadcast_to(rstd, (span, LANES))
    second[...] = (normed * vec(5) + vec(6)).astype(BF16)
    racc[...] = jnp.zeros_like(racc)
    dsec[...] = jnp.zeros_like(dsec)
    for copy in load_1:
        copy.wait()
    load_2.wait()
    curve = math.sqrt(2.0 / math.pi)

    def feed(t, carry):
        w2_rows = pl.ds(pl.multiple_of(t * tile, tile), tile)
        pre = dot(second[...], w1[t]) + inb_ref[pl.ds(t, 1), :]
        square = pre * pre
        bend = jnp.tanh(curve * (pre + 0.044715 * (square * pre)))
        half = 0.5 * (1.0 + bend)
        act = (pre * half).astype(BF16)
        slope = half + 0.5 * pre * (1.0 - bend * bend) * (curve * (1.0 + 3 * 0.044715 * square))
        upstream = up[...]
        racc[...] += dot(act, w2[w2_rows])
        d_pre = (dot_nt(upstream, w2[w2_rows]) * slope).astype(BF16)
        base = (t // 2) * 4 * tile + (t % 2) * tile
        grads[rows_at(base, tile)] = dot_tn(act, upstream).astype(BF16)
        grads[rows_at(base + 2 * tile, tile)] = dot_tn(second[...], d_pre).astype(BF16)
        vstage[0, pl.ds(V_INNB + t, 1), :] = total(d_pre.astype(F32))
        dsec[...] += dot_nt(d_pre, w1[t])

        @pl.when(t == 1)
        def _():
            part_a[0]()

        return carry

    lax.fori_loop(0, tiles, feed, 0)
    out_ref[0] = (mid[...] + racc[...] + vec(7)).astype(BF16)

    up_f = up[...].astype(F32)
    vstage[0, V_OUTB : V_OUTB + 1] = total(up_f)
    d_second, normed = dsec[...], n2[...]
    scaled = d_second * vec(5)
    vstage[0, V_MIDG : V_MIDG + 1] = total(d_second * normed)
    vstage[0, V_MIDS : V_MIDS + 1] = total(d_second)
    d_mid = up_f + (scaled - mean(scaled) - normed * mean(scaled * normed)) * stats[1][:, :1]
    mid[...] = d_mid
    d_branch = d_mid.astype(BF16)
    vstage[0, V_OB : V_OB + 1] = total(d_branch.astype(F32))
    grads[2 * hidden : 2 * hidden + width] = dot_tn(att[...], d_branch).astype(BF16)
    part_b[0]()
    d_att = dot_nt(d_branch, wo[...]).astype(BF16)
    for b in range(pairs):
        dah[b] = d_att[:, b * LANES : (b + 1) * LANES]

    schedule = {
        0: [part_a[1]],
        1: [part_b[1]],
        3: [part_a[2]],
        5: [part_b[2], part_a[3]],
        7: [part_a[4], part_b[3]],
    }

    def attend_back(i, carry):
        c, b = i // pairs, i % pairs
        q2 = two_heads(qh[b, chunk_rows(c)])
        g2 = two_heads(dah[b, chunk_rows(c)])
        low = probs[i]
        prob = low.astype(F32)
        d_prob = dot_nt(g2, slots[c, pairs + b])
        weighted = prob * d_prob
        d_score = (weighted - prob * jnp.sum(weighted, axis=1, keepdims=True)).astype(BF16)
        d_query = merge_heads(dot(d_score, slots[c, b])) * (1.0 / math.sqrt(HEAD_DIM))
        dq[chunk_rows(c), pair_lanes(b)] = d_query.astype(BF16)
        dslots[c, b] = dot_tn(d_score, q2)
        dslots[c, pairs + b] = dot_tn(low, g2)
        for when, steps in schedule.items():

            @pl.when(i == when)
            def _():
                sequence(*steps)

        return carry

    lax.fori_loop(0, plan.chunks * pairs, attend_back, 0)

    def fold(b, carry):
        for c in range(plan.chunks):
            for s0, kind, at, n in slot_pieces(c):
                piece = dslots[c, b, s0 : s0 + n]
                if kind == "own":
                    parts_done = own_done[c].get((s0, at))
                    seen = parts_done if parts_done is not None else 0
                    if seen:
                        own[b, at : at + seen] += piece[:seen]
                    if seen < n:
                        own[b, at + seen : at + n] = piece[seen:]
                elif own_done[c].get((s0, kind)):
                    side = 0 if kind == "low" else 1
                    hsend[side, b, at : at + n] = (
                        hsend[side, b, at : at + n].astype(F32) + piece
                    ).astype(BF16)
                else:
                    side = 0 if kind == "low" else 1
                    hsend[side, b, at : at + n] = piece.astype(BF16)
        far = dslots[0, b, plan.far_slot :]
        for c in range(1, plan.chunks):
            far = far + dslots[c, b, plan.far_slot :]
        back = dot_tn(select, far.astype(BF16))
        for s in range(seq):
            fsend[s, b] = back[s * NR : (s + 1) * NR].astype(BF16)
        return carry

    own_done = []
    reached, halo_seen = {}, set()
    for c in range(plan.chunks):
        done = {}
        for s0, kind, at, n in slot_pieces(c):
            if kind == "own":
                lv = max(v for v in range(near + 1) if level_start(v) <= at)
                limit = reached.get(lv, level_start(lv))
                done[(s0, at)] = max(0, min(limit, at + n) - at)
                reached[lv] = max(limit, at + n)
            else:
                done[(s0, kind)] = (kind, at) in halo_seen
                halo_seen.add((kind, at))
        own_done.append(done)

    lax.fori_loop(0, blocks, fold, 0)

    def far_back(k):
        other, device = peer(3, k)
        return remote(
            fsend.at[other], frecv.at[k - 1], fback_send.at[k - 1], fback_recv.at[k - 1], device
        )

    halo_start(hsend, hrecv, back_send, back_recv)
    for k in range(1, seq):
        far_back(k).start()

    d_query = dq[...]
    vstage[0, V_QB : V_QB + 1] = total(d_query.astype(F32))
    off_c = plan.parts[2][0]
    grads[off_c : off_c + width] = dot_tn(first[...], d_query).astype(BF16)
    d_first = dot_nt(d_query, wq[...])
    racc[...] = d_first
    sequence(part_b[4], part_a[5])

    spread = averaging(1)
    halo_wait(hsend, hrecv, back_send, back_recv)
    for k in range(1, seq):
        far_back(k).wait()
    for lv in range(near + 1):
        at, n = level_start(lv), span >> lv
        lo, hi = lv * NR, (lv + 1) * NR
        own[:, at : at + NR] += hrecv[0, :, lo:hi].astype(F32)
        own[:, at + n - NR : at + n] += hrecv[1, :, lo:hi].astype(F32)
    far_sum = fsend[seq_id].astype(F32)
    for k in range(1, seq):
        far_sum = far_sum + frecv[k - 1].astype(F32)
    for b in range(blocks):
        cols = slice(b * LANES, (b + 1) * LANES)
        coarse[:far_at, cols] = own[b, span : span + far_at].astype(BF16)
        coarse[far_at:, cols] = far_sum[b].astype(BF16)
    for half in range(2):
        passed = dot(spread, coarse[:, half * width : (half + 1) * width])
        for b in range(pairs):
            cols = slice((half * pairs + b) * LANES, (half * pairs + b + 1) * LANES)
            dkv[:, cols] = (
                own[half * pairs + b, :span] + passed[:, b * LANES : (b + 1) * LANES]
            ).astype(BF16)
    d_keys, d_values = dkv[:, :width], dkv[:, width:]
    vstage[0, V_VB : V_VB + 1] = total(d_values.astype(F32))
    grads[off_c + width : off_c + 2 * width] = dot_tn(first[...], d_keys).astype(BF16)
    grads[off_c + 2 * width : off_c + 3 * width] = dot_tn(first[...], d_values).astype(BF16)
    part_c[0]()

    d_first = racc[...] + dot_nt(d_keys, wk[...]) + dot_nt(d_values, wv[...])
    normed = n1[...]
    scaled = d_first * vec(0)
    vstage[0, V_PREG : V_PREG + 1] = total(d_first * normed)
    vstage[0, V_PRES : V_PRES + 1] = total(d_first)
    d_in = mid[...] + (scaled - mean(scaled) - normed * mean(scaled * normed)) * stats[0][:, :1]
    gin_ref[0] = d_in.astype(BF16)

    vec_received = [vrecv0, vrecv1, vrecv2, vrecv3]

    def vec_copy(digit, k):
        _, device = peer(digit, k)
        return remote(
            vstage.at[digit], vec_received[digit].at[index[digit]],
            vec_send.at[digit, k - 1], vec_recv.at[digit, k - 1], device,
        )

    def vec_start(digit):
        for k in range(1, count[digit]):
            vec_copy(digit, k).start()

    def vec_finish(digit):
        for k in range(1, count[digit]):
            vec_copy(digit, k).wait_recv()
        acc = jnp.zeros((VEC_ROWS, width), F32)
        for s in range(count[digit]):
            acc = acc + jnp.where(index[digit] == s, vstage[digit], vec_received[digit][s])
        if digit == 3:
            vout_ref[...] = acc
        else:
            vstage[digit + 1] = acc

    vec_start(0)

    part_c[1]()
    part_b[5]()
    vec_finish(0)
    vec_start(1)
    part_a[6]()
    part_c[2]()
    vec_finish(1)
    vec_start(2)
    part_b[6]()
    part_c[3]()
    vec_finish(2)
    vec_start(3)
    part_a[7]()
    part_c[4]()
    part_b[7]()
    part_c[5]()
    part_c[6]()
    vec_finish(3)
    part_a[8]()
    part_c[7]()
    part_b[8]()
    part_c[8]()

    for part in range(3):
        for digit in range(4):
            for k in range(1, count[digit]):
                rs_copy(part, digit, k).wait_send()
                if digit < 3 or plan.scatter[part]:
                    ag_copy(part, digit, k).wait_send()
    for digit in range(4):
        for k in range(1, count[digit]):
            vec_copy(digit, k).wait_send()


def unpack_kernel(
    width, tiles, red_hbm, vec_ref,
    query_ref, key_ref, value_ref, output_ref, inner_ref, outer_ref,
    preg_ref, pres_ref, qb_ref, vb_ref, ob_ref, midg_ref, mids_ref, outb_ref, innb_ref,
    low, wide, in_sem, out_sem,
):
    targets = []
    for t in range(tiles):
        at = (t // 2) * 4 + t % 2
        rows = slice(t * width, (t + 1) * width)
        targets.append((at, outer_ref.at[rows]))
        targets.append((at + 2, inner_ref.at[:, rows]))
    for i, ref in enumerate((output_ref, query_ref, key_ref, value_ref)):
        targets.append((2 * tiles + i, ref))

    def fetch(i):
        at = targets[i][0]
        return pltpu.make_async_copy(
            red_hbm.at[at * width : (at + 1) * width], low.at[i % 4], in_sem.at[i % 4]
        )

    def put(i):
        return pltpu.make_async_copy(wide.at[i % 4], targets[i][1], out_sem.at[i % 4])

    n = len(targets)
    for i in range(min(3, n)):
        fetch(i).start()
    for row, ref in (
        (V_PREG, preg_ref), (V_PRES, pres_ref), (V_QB, qb_ref), (V_VB, vb_ref), (V_OB, ob_ref),
        (V_MIDG, midg_ref), (V_MIDS, mids_ref), (V_OUTB, outb_ref),
    ):
        ref[...] = vec_ref[row]
    for t in range(tiles):
        innb_ref[t * width : (t + 1) * width] = vec_ref[V_INNB + t]
    for i in range(n):
        fetch(i).wait()
        if i >= 4:
            put(i - 4).wait()
        wide[i % 4] = low[i % 4].astype(F32)
        put(i).start()
        if i + 3 < n:
            fetch(i + 3).start()
    for i in range(max(0, n - 4), n):
        put(i).wait()


def shards(
    rows, seq,
    tokens, segment_ids, prenorm_gain, prenorm_shift, query_proj, query_bias, key_proj, value_proj,
    value_bias, output_proj, output_bias, midnorm_gain, midnorm_shift, inner_proj, inner_bias,
    outer_proj, outer_bias, upstream,
):
    _, span, width = tokens.shape
    hidden = inner_proj.shape[1]
    plan = Plan(rows, seq, span, width, hidden)
    tiles = hidden // width
    pairs = width // LANES
    vectors = jnp.concatenate(
        [
            prenorm_gain, prenorm_shift, query_bias, value_bias, output_bias, midnorm_gain,
            midnorm_shift, outer_bias,
        ]
    ).reshape(8, width)
    count = plan.counts
    most = max(count) - 1
    vmem = pl.BlockSpec(memory_space=pltpu.VMEM)
    hbm = pl.BlockSpec(memory_space=pl.ANY)
    grad_rows = plan.grad_rows
    rest = [grad_rows // 2, grad_rows // 4, grad_rows // 4 // count[2]]
    last = rest[2] // seq if all(plan.scatter) else rest[2]
    dma = pltpu.SemaphoreType.DMA
    items = plan.chunks * pairs
    scratch = [
        pltpu.VMEM((span, width), BF16),
        pltpu.VMEM((span, width), BF16),
        pltpu.VMEM((width, width), BF16),
        pltpu.VMEM((width, width), BF16),
        pltpu.VMEM((width, width), BF16),
        pltpu.VMEM((width, width), BF16),
        pltpu.VMEM((tiles, width, width), BF16),
        pltpu.VMEM((hidden, width), BF16),
        pltpu.VMEM((span, width), F32),
        pltpu.VMEM((span, width), F32),
        pltpu.VMEM((span, width), F32),
        pltpu.VMEM((span, width), F32),
        pltpu.VMEM((span, width), F32),
        pltpu.VMEM((span, width), BF16),
        pltpu.VMEM((span, width), BF16),
        pltpu.VMEM((pairs, span, LANES), BF16),
        pltpu.VMEM((span, width), BF16),
        pltpu.VMEM((pairs, span, LANES), BF16),
        pltpu.VMEM((span, width), BF16),
        pltpu.VMEM((2 * pairs, span + plan.far_row, LANES), BF16),
        pltpu.VMEM((2, 2 * pairs, plan.edge, LANES), BF16),
        pltpu.VMEM((2, 2 * pairs, plan.edge, LANES), BF16),
        pltpu.VMEM((seq, NR, 2 * width), BF16),
        pltpu.VMEM((plan.chunks, 2 * pairs, plan.slots, LANES), BF16),
        pltpu.VMEM((seq, 8, span), BF16),
        pltpu.VMEM((plan.chunks, plan.chunk, plan.slots), F32),
        pltpu.VMEM((items, 2 * plan.chunk, plan.slots), BF16),
        pltpu.VMEM((plan.chunks, 2 * pairs, plan.slots, LANES), F32),
        pltpu.VMEM((2 * pairs, span + plan.far_row, LANES), F32),
        pltpu.VMEM((2, 2 * pairs, plan.edge, LANES), BF16),
        pltpu.VMEM((2, 2 * pairs, plan.edge, LANES), BF16),
        pltpu.VMEM((seq, 2 * pairs, NR, LANES), BF16),
        pltpu.VMEM((seq - 1, 2 * pairs, NR, LANES), BF16),
        pltpu.VMEM((plan.coarse_rows, 2 * width), BF16),
        pltpu.VMEM((span, 2 * width), BF16),
        pltpu.VMEM((grad_rows, width), BF16),
        pltpu.VMEM((count[0] - 1, rest[0], width), BF16),
        pltpu.VMEM((count[1] - 1, rest[1], width), BF16),
        pltpu.VMEM((count[2] - 1, rest[2], width), BF16),
        pltpu.VMEM((count[3] - 1, last, width), BF16),
        pltpu.VMEM((4, VEC_ROWS, width), F32),
        pltpu.VMEM((count[0], VEC_ROWS, width), F32),
        pltpu.VMEM((count[1], VEC_ROWS, width), F32),
        pltpu.VMEM((count[2], VEC_ROWS, width), F32),
        pltpu.VMEM((count[3], VEC_ROWS, width), F32),
        pltpu.VMEM((2, span, LANES), F32),
        dma((7 + tiles,)),
        dma((2,)), dma((2,)),
        dma((seq - 1,)), dma((seq - 1,)),
        dma((2,)), dma((2,)),
        dma((seq - 1,)), dma((seq - 1,)),
        dma((3, 4, most)), dma((3, 4, most)),
        dma((3, 4, most)), dma((3, 4, most)),
        dma((4, most)), dma((4, most)),
    ]
    layer_output, input_grad, reduced, vecs = pl.pallas_call(
        functools.partial(layer_kernel, plan),
        out_shape=(
            jax.ShapeDtypeStruct(tokens.shape, BF16),
            jax.ShapeDtypeStruct(tokens.shape, BF16),
            jax.ShapeDtypeStruct((grad_rows, width), BF16),
            jax.ShapeDtypeStruct((VEC_ROWS, width), F32),
        ),
        in_specs=[hbm, vmem, vmem, vmem] + [hbm] * 7,
        out_specs=(vmem, vmem, vmem, vmem),
        scratch_shapes=scratch,
        compiler_params=pltpu.CompilerParams(
            collective_id=0, has_side_effects=True, vmem_limit_bytes=60 * 1024 * 1024
        ),
        name="layer",
    )(
        tokens, segment_ids, vectors, inner_bias.reshape(tiles, width), query_proj, key_proj,
        value_proj, output_proj, inner_proj, outer_proj, upstream,
    )
    matrix = jax.ShapeDtypeStruct((width, width), F32)
    vector = jax.ShapeDtypeStruct((width,), F32)
    grads = pl.pallas_call(
        functools.partial(unpack_kernel, width, tiles),
        out_shape=(
            matrix, matrix, matrix, matrix,
            jax.ShapeDtypeStruct((width, hidden), F32),
            jax.ShapeDtypeStruct((hidden, width), F32),
            vector, vector, vector, vector, vector, vector, vector, vector,
            jax.ShapeDtypeStruct((hidden,), F32),
        ),
        in_specs=[hbm, vmem],
        out_specs=(hbm,) * 6 + (vmem,) * 9,
        scratch_shapes=[
            pltpu.VMEM((4, width, width), BF16),
            pltpu.VMEM((4, width, width), F32),
            dma((4,)), dma((4,)),
        ],
        name="unpack",
    )(reduced, vecs)
    (query_g, key_g, value_g, output_g, inner_g, outer_g,
     preg, pres, qb, vb, ob, midg, mids, outb, innb) = grads
    return (
        layer_output, input_grad, preg, pres, query_g, qb, key_g, value_g, vb, output_g, ob,
        midg, mids, inner_g, innb, outer_g, outb,
    )


def solution(mesh):
    split, ids, whole = P("rows", "seq", None), P("rows", "seq"), P()
    in_specs = (split, ids) + (whole,) * 15 + (split,)
    out_specs = (split, split) + (whole,) * 15
    return jax.shard_map(
        functools.partial(shards, mesh.shape["rows"], mesh.shape["seq"]),
        mesh=mesh, in_specs=in_specs, out_specs=out_specs, check_vma=False,
    )
```

time: 1130 us -> 146 us (0.13); the launches traced: 1110 us -> 144 us
  local copies, waits for them, and re-layouts: 620 us -> 8.82 us
  waiting for transfers between devices: 164 us -> 0 us
  Pallas kernels: 0 us -> 134 us
  matrix products: 100 us -> 0 us
  other arithmetic: 80.5 us -> 0.01 us
  blocking collectives: 68.3 us -> 0 us
  starting transfers between devices: 62.2 us -> 0 us
  between operations: 17.2 us -> 0.7 us
    gather x12 -> x0, local copies, waits for them, and re-layouts: 352 us -> none  [level_mask(): jnp.take(coarse_ids, jnp.clip(key_index, 0, coarse_count - 1), axis=1)]
    psum x1 -> x0, waiting for transfers between devices: 164 us -> none  [shards(): lax.psum((prenorm_gain_gradient, prenorm_shift_gradient, query_grad, quer...]
    pallas_call x0 -> x2, Pallas kernels: none -> 134 us  [the longest x1 125 us: shards(): pl.pallas_call(functools.partial(layer_kernel, plan), out_shape=(jax.Shap...]
    dot_general x54 -> x0, matrix products: 100 us -> none  [the longest x6 15.7 us: shards(): jnp.einsum('rbqhd,rbkhd->rbqhk', grad_blocks, value_window, preferred_ele...]
    reshape x34 -> x2, local copies, waits for them, and re-layouts: 69 us -> 1.91 us  [the longest x1 1.3 us: shards(): inner_bias.reshape(tiles, width)]
    ppermute x20 -> x0, starting transfers between devices: 62.1 us -> none  [the longest x10 49.3 us: with_halo(): lax.ppermute(lax.slice_in_dim(block, block.shape[dim] - width, None, axis...]
    psum x1 -> x0, blocking collectives: 43 us -> none  [shards(): lax.psum((prenorm_gain_gradient, prenorm_shift_gradient, query_grad, quer...]
    another operation x20 -> x0, local copies, waits for them, and re-layouts: 40.9 us -> none
  transfers between devices with their start and end apart: 22 -> 0, of which waited for: 1 -> 0; matrix products, arithmetic and copies ran while one was open for 45% -> 0% of each run, Pallas kernels for 0% -> 0%
where the time goes in v1:
time: 146 us; the launch traced here: 144 us
  Pallas kernels  134 us (92%)
  local copies, waits for them, and re-layouts  8.82 us (6%)
    pallas_call x1, Pallas kernels, shards(): pl.pallas_call(functools.partial(layer_kernel, plan), out_shape=(jax.Shap...  125 us
    pallas_call x1, Pallas kernels, shards(): pl.pallas_call(functools.partial(unpack_kernel, width, tiles), out_shape=...  9.25 us
    unnamed x13, local copies, waits for them, and re-layouts  6.22 us

profile of v1, /device:TPU:0, one launch (start us, length us, event | category | flops | bytes accessed | tf_op | source)
XLA Modules:
  0.0 143.7 jit_solution(17336640490594786997)
XLA Ops:
  0.7 1.3 reshape.41.inb_ref
  2.0 0.7 constant_dynamic-update-slice_fusion.7
  2.6 0.7 constant_dynamic-update-slice_fusion.6
  3.3 0.7 constant_dynamic-update-slice_fusion.5
  4.0 0.7 constant_dynamic-update-slice_fusion.4
  4.7 0.7 constant_dynamic-update-slice_fusion.3
  5.4 0.7 constant_dynamic-update-slice_fusion.2
  6.1 0.7 constant_dynamic-update-slice_fusion.1
  6.8 0.7 constant_dynamic-update-slice_fusion
  7.5 0.6 reshape.40.vec_ref
  8.1 124.9 %layer.1 = (bf16[1,256,512]{2,1,0:T(8,128)(2,1)}, bf16[1,256,512]{2,1,0:T(8,128)(2,1)}, bf16[6144,512]{1,0:T(8,128)(2,1)}, f32[16,512]{1,0:T(8,128)}) custom-call(bf16[1,256,512]{2,1,0:T(8,128)(2,1)} %tok_hbm.1, s32[1,256]{1,0:T(1,128)} %ids_ref.1, f32[8,512]{1,0:T(8,128)} %reshape.40.vec_ref, f32[4,512]{1,0:T(4,128)} %reshape.41.inb_ref, ...), custom_call_target="tpu_custom_call" | custom-call | tf_op jit(solution)/shard_map/layer/pallas_call | solution.py:895
  133.0 0.0 copy-start.1
  133.0 0.0 copy-start
  133.0 9.3 %unpack.1 = (f32[512,512]{1,0:T(8,128)}, f32[512,512]{1,0:T(8,128)}, f32[512,512]{1,0:T(8,128)}, f32[512,512]{1,0:T(8,128)}, f32[512,2048]{1,0:T(8,128)}, /*inde...) custom-call(bf16[6144,512]{1,0:T(8,128)(2,1)} %get-tuple-element.38., ...), custom_call_target="tpu_custom_call" | custom-call | tf_op jit(solution)/shard_map/unpack/pallas_call | solution.py:916
  142.2 0.0 copy-done.1
  142.3 0.7 copy.45
  143.0 0.0 copy-done
  143.0 0.7 copy.46
  (1 shorter events, 0.0 us)
Async XLA Ops:
  133.0 9.3 %copy-start.1 = (bf16[1,256,512]{2,1,0:T(8,128)(2,1)S(1)}, bf16[1,256,512]{2,1,0:T(8,128)(2,1)}, u32[]{:S(2)}) copy-start(bf16[1,256,512]{2,1,0:T(8,128)(2,1)} %get-tuple-element.72) | copy-start | bytes 786436
  133.0 10.0 %copy-start = (bf16[1,256,512]{2,1,0:T(8,128)(2,1)S(1)}, bf16[1,256,512]{2,1,0:T(8,128)(2,1)}, u32[]{:S(2)}) copy-start(bf16[1,256,512]{2,1,0:T(8,128)(2,1)} %get-tuple-element.73) | copy-start | bytes 786436

commit v2 on v1

--- a/solution.py
+++ b/solution.py
@@ -66,7 +66,6 @@
             self.level_row.append(at)
             at += span >> level
         self.coarse_rows = self.far_row + NR
-        self.id_row = NR - 2
         self.slot, self.slot_len = [], []
         at = 0
         for level in range(self.top + 1):
@@ -80,14 +79,10 @@
         self.far_slots = self.slots - self.far_slot
         self.edge = NR * (self.near + 1)
         self.grad_rows = 4 * width + 2 * hidden
-        ffn = hidden
-        self.parts = [(0, ffn), (ffn, ffn + width), (2 * ffn + width, 3 * width)]
+        self.parts = [(p * 2 * width, 2 * width) for p in range(self.grad_rows // (2 * width))]
         self.counts = [2, 2, rows // 4, seq]
         self.swap = rows // 4 == 2
-        self.scatter = []
-        for off, n in self.parts:
-            per = n // (2 * 2 * (rows // 4))
-            self.scatter.append(per % (NR * seq) == 0)
+        self.scatter = (2 * width // rows) % (NR * seq) == 0
 
 
 def sequence(*steps):
@@ -97,12 +92,14 @@
 
 def layer_kernel(
     plan,
-    tok_hbm, ids_ref, vec_ref, inb_ref, wq_hbm, wk_hbm, wv_hbm, wo_hbm, w1_hbm, w2_hbm, up_hbm,
-    out_ref, gin_ref, red_ref, vout_ref,
+    tok_hbm, ids_ref, preg_ref, pres_ref, wq_hbm, qb_ref, wk_hbm, wv_hbm, vb_ref, wo_hbm, ob_ref,
+    midg_ref, mids_ref, w1_hbm, inb_ref, w2_hbm, outb_ref, up_hbm,
+    out_ref, gin_ref, red_hbm, vout_ref,
     tok, up, wq, wk, wv, wo, w1, w2, n1, n2, mid, racc, dsec, first, second, qh, att, dah, dq,
-    level, edge, halo, farg, slots, levs, bias, probs, dslots, own, hsend, hrecv, fsend, frecv,
-    coarse, dkv, grads, recv0, recv1, recv2, recv3, vstage, vrecv0, vrecv1, vrecv2, vrecv3, stats,
-    in_sem, halo_send, halo_recv, far_send, far_recv, back_send, back_recv, fback_send, fback_recv,
+    level, edge, halo, farg, slots, bias, probs, dslots, own, hsend, hrecv, fsend, frecv,
+    coarse, spread, dkv, grads, recv0, recv1, recv2, recv3, vstage, vrecv0, vrecv1, vrecv2, vrecv3, stats,
+    inb, red_ref,
+    in_sem, out_sem, halo_send, halo_recv, far_send, far_recv, back_send, back_recv, fback_send, fback_recv,
     rs_send, rs_recv, ag_send, ag_recv, vec_send, vec_recv,
 ):
     span, width, hidden = plan.span, plan.width, plan.hidden
@@ -160,6 +157,8 @@
     halo[...] = jnp.zeros_like(halo)
     hrecv[...] = jnp.zeros_like(hrecv)
     vstage[0] = jnp.zeros((VEC_ROWS, width), F32)
+    for t in range(tiles):
+        inb[t : t + 1, :] = inb_ref[t * tile : (t + 1) * tile].reshape(1, tile)
 
     barrier = pltpu.get_barrier_semaphore()
     greeted = 0
@@ -169,8 +168,10 @@
             pl.semaphore_signal(barrier, inc=1, device_id=device, device_id_type=MESH)
             greeted += 1
 
+    vectors = (preg_ref, pres_ref, qb_ref, vb_ref, ob_ref, midg_ref, mids_ref, outb_ref)
+
     def vec(row):
-        return vec_ref[row : row + 1, :]
+        return vectors[row][...].reshape(1, width)
 
     load_tok.wait()
     x = tok[...].astype(F32)
@@ -199,19 +200,22 @@
         return matrix.astype(BF16)
 
     matrix = averaging(0)
-    ids_f = ids_ref[...].astype(F32)
-    ids_wide = jnp.concatenate([ids_f, jnp.zeros((1, 2 * width - span), F32)], axis=1)
     far_at = plan.far_row
+    feature = (iota((LANES, span), 0) == ids_ref[...]).astype(F32).astype(BF16)
+    unit = (iota((span, span), 0) == iota((span, span), 1)).astype(F32).astype(BF16)
+    id_hot = dot_nt(unit, feature).astype(BF16)
+    level[blocks, :span] = id_hot
     for half, kv in enumerate((keys, values)):
-        mixed = dot(matrix, kv)
+        mixed = dot(matrix, kv).astype(BF16)
         for b in range(pairs):
             level[half * pairs + b, span : span + far_at] = mixed[
                 :far_at, b * LANES : (b + 1) * LANES
-            ].astype(BF16)
-        ids_half = jnp.broadcast_to(ids_wide[:, half * width : (half + 1) * width], (NR, width))
-        farg[seq_id, :, half * width : (half + 1) * width] = jnp.where(
-            iota((NR, width), 0) == plan.id_row, ids_half, mixed[far_at:]
-        ).astype(BF16)
+            ]
+        farg[seq_id, :, half * width : (half + 1) * width] = mixed[far_at:]
+    alike = dot(matrix, id_hot)
+    alike = jnp.where((alike > 0.999) & (iota(alike.shape, 1) > 0), 1.0, 0.0).astype(BF16)
+    level[blocks, span : span + far_at] = alike[:far_at]
+    farg[seq_id, :, 2 * width :] = alike[far_at:]
 
     def level_start(lv):
         return 0 if lv == 0 else span + plan.level_row[lv]
@@ -289,48 +293,6 @@
                 pieces.append((s0, "high", lv * NR, NR))
         return pieces
 
-    halo_wait(edge, halo, halo_send, halo_recv)
-    for c in range(plan.chunks):
-        for s0, kind, at, n in slot_pieces(c):
-            if kind == "own":
-                slots[c, :, s0 : s0 + n] = level[:, at : at + n]
-            else:
-                slots[c, :, s0 : s0 + n] = halo[0 if kind == "low" else 1, :, at : at + n]
-    for k in range(1, seq):
-        far_copy(k).wait()
-
-    def far_select():
-        pieces = []
-        for lv in plan.far:
-            per_log = (span >> lv).bit_length() - 1
-            first_row = plan.level_row[lv] - plan.far_row
-            j = (start // (NR << lv) - 1) * NR + iota((3 * NR, seq * NR), 0)
-            column = (j >> per_log) * NR + (j & ((1 << per_log) - 1)) + first_row
-            pieces.append((column == iota((3 * NR, seq * NR), 1)).astype(F32))
-        rest = plan.far_slots - 3 * NR * len(plan.far)
-        if rest:
-            pieces.append(jnp.zeros((rest, seq * NR), F32))
-        return jnp.concatenate(pieces, axis=0).astype(BF16)
-
-    select = far_select()
-    far_values = dot(select, farg[...].reshape(seq * NR, 2 * width)).astype(BF16)
-    for c in range(plan.chunks):
-        for b in range(blocks):
-            slots[c, b, plan.far_slot :] = far_values[:, b * LANES : (b + 1) * LANES]
-
-    row_ids = [farg[s].astype(F32)[plan.id_row : plan.id_row + 1, :span] for s in range(seq)]
-    current = jnp.concatenate(row_ids, axis=1)
-    level_ids = [current]
-    for lv in range(1, top + 1):
-        shifted = pltpu.roll(current, plan.length - (1 << (lv - 1)), 1)
-        current = jnp.where(current == shifted, current, 0.0)
-        level_ids.append(current)
-    level_ids += [jnp.zeros_like(current)] * (8 - len(level_ids))
-    stacked = jnp.concatenate(level_ids, axis=0).astype(BF16)
-    for s in range(seq):
-        levs[s] = stacked[:, s * span : (s + 1) * span]
-
-    ids_rows = jnp.broadcast_to(ids_f, (8, span)).astype(BF16)
     slot_at = iota((1, plan.slots), 1)
     slot_level = jnp.zeros((1, plan.slots), jnp.int32)
     for lv in range(1, top + 1):
@@ -345,27 +307,45 @@
                 base = (origin // (NR << lv) - 1) * NR
             here = slot_at - plan.slot[lv] + base
             j = here if lv == 0 else jnp.where(slot_level == lv, here, j)
-        j = jnp.where(slot_at < plan.used, j, -1)
-        goal = j << slot_level
-
-        def gather_ids(s, found):
-            hot = iota((span, plan.slots), 0) + s * span == goal
-            return found + dot(levs[s], hot.astype(F32).astype(BF16))
-
-        found = lax.fori_loop(0, seq, gather_ids, jnp.zeros((8, plan.slots), F32))
-        own_level = iota((8, plan.slots), 0) == slot_level
-        key_id = jnp.sum(jnp.where(own_level, found, 0.0), axis=0, keepdims=True)
-        mine = (iota((plan.chunk, span), 1) == iota((plan.chunk, span), 0) + c * plan.chunk)
-        query_id = dot_nt(mine.astype(F32).astype(BF16), ids_rows)[:, :1]
-        inside = (goal >= 0) & (goal < plan.length) & (j >= 0)
-        usable = inside & ((slot_level == 0) | (key_id > 0.5))
-        key_id = jnp.where(usable, key_id, -1.0)
         position = origin + iota((plan.chunk, plan.slots), 0)
         off_block = (j >> 4) - (position >> (slot_level + 4))
         off_half = (j >> 3) - (position >> (slot_level + 3))
         reach = jnp.where(slot_level == 0, -1, 1)
-        counted = (key_id == query_id) & (jnp.abs(off_block) <= 1) & (jnp.abs(off_half) > reach)
-        bias[c] = jnp.where(counted, slot_level.astype(F32) * LOG_TWO, MASKED)
+        within = (jnp.abs(off_block) <= 1) & (jnp.abs(off_half) > reach)
+        bias[c] = jnp.where(within, slot_level.astype(F32) * LOG_TWO, MASKED)
+
+    def far_select():
+        pieces = []
+        for lv in plan.far:
+            per_log = (span >> lv).bit_length() - 1
+            first_row = plan.level_row[lv] - plan.far_row
+            j = (start // (NR << lv) - 1) * NR + iota((3 * NR, seq * NR), 0)
+            column = (j >> per_log) * NR + (j & ((1 << per_log) - 1)) + first_row
+            pieces.append((column == iota((3 * NR, seq * NR), 1)).astype(F32))
+        rest = plan.far_slots - 3 * NR * len(plan.far)
+        if rest:
+            pieces.append(jnp.zeros((rest, seq * NR), F32))
+        return jnp.concatenate(pieces, axis=0).astype(BF16)
+
+    select = far_select()
+    spread[...] = averaging(1)
+
+    halo_wait(edge, halo, halo_send, halo_recv)
+    for c in range(plan.chunks):
+        for s0, kind, at, n in slot_pieces(c):
+            if kind == "own":
+                slots[c, :, s0 : s0 + n] = level[:, at : at + n]
+            else:
+                slots[c, :, s0 : s0 + n] = halo[0 if kind == "low" else 1, :, at : at + n]
+    for k in range(1, seq):
+        far_copy(k).wait()
+    far_values = dot(select, farg[...].reshape(seq * NR, 2 * width + LANES)).astype(BF16)
+    for c in range(plan.chunks):
+        for b in range(blocks + 1):
+            slots[c, b, plan.far_slot :] = far_values[:, b * LANES : (b + 1) * LANES]
+    for c in range(plan.chunks):
+        same = dot_nt(level[blocks, c * plan.chunk : (c + 1) * plan.chunk], slots[c, blocks])
+        bias[c] = jnp.where(same > 0.5, bias[c], MASKED)
 
     lane = iota((1, LANES), 1)
     low_half = (lane < HEAD_DIM).astype(F32).astype(BF16)
@@ -400,12 +380,10 @@
     lax.fori_loop(0, plan.chunks * pairs, attend, 0)
 
     received = [recv0, recv1, recv2, recv3]
-    starts = [recv0.shape[1], recv1.shape[1], recv2.shape[1], recv3.shape[1]]
-    step_of_part = []
 
     def region(part, digits):
-        off, n = plan.parts[part]
-        base = off
+        n = plan.parts[0][1]
+        base = part * n
         for digit in range(digits):
             n = n // count[digit]
             base = base + index[digit] * n
@@ -414,24 +392,22 @@
     def rows_at(base, n):
         return pl.ds(pl.multiple_of(base, NR), n)
 
-    def received_rows(part, digit, n):
-        off, whole = plan.parts[part]
-        share = whole // n
-        return pl.ds(off // share, n)
+    def received_rows(part, n):
+        return rows_at(part * n, n)
 
     def rs_copy(part, digit, k):
         base, n = region(part, digit)
         other, device = peer(digit, k)
-        if digit == 3 and not plan.scatter[part]:
+        if digit == 3 and not plan.scatter:
             return remote(
                 grads.at[rows_at(base, n)],
-                received[digit].at[k - 1, received_rows(part, digit, n)],
+                received[digit].at[k - 1, received_rows(part, n)],
                 rs_send.at[part, digit, k - 1], rs_recv.at[part, digit, k - 1], device,
             )
         n = n // count[digit]
         return remote(
             grads.at[rows_at(base + other * n, n)],
-            received[digit].at[k - 1, received_rows(part, digit, n)],
+            received[digit].at[k - 1, received_rows(part, n)],
             rs_send.at[part, digit, k - 1], rs_recv.at[part, digit, k - 1], device,
         )
 
@@ -442,10 +418,9 @@
     def rs_finish(part, digit):
         for k in range(1, count[digit]):
             rs_copy(part, digit, k).wait_recv()
-        gather_all = digit == 3 and not plan.scatter[part]
+        gather_all = digit == 3 and not plan.scatter
         base, n = region(part, digit if gather_all else digit + 1)
-        off, whole = plan.parts[part]
-        at = off // (whole // n)
+        at = part * n
         target = red_ref if digit == 3 else grads
         block = 64 if n % 64 == 0 else NR
 
@@ -476,19 +451,19 @@
         )
 
     def ag_start(part, digit):
-        if digit == 3 and not plan.scatter[part]:
+        if digit == 3 and not plan.scatter:
             return
         for k in range(1, count[digit]):
             ag_copy(part, digit, k).start()
 
     def ag_finish(part, digit):
-        if digit == 3 and not plan.scatter[part]:
+        if digit == 3 and not plan.scatter:
             return
         for k in range(1, count[digit]):
             ag_copy(part, digit, k).wait_recv()
 
     def part_steps(part):
-        steps = [lambda: rs_start(part, 0)]
+        steps = [functools.partial(rs_start, part, 0)]
         for digit in range(1, 4):
             steps.append(
                 functools.partial(
@@ -510,10 +485,22 @@
                     functools.partial(ag_start, part, digit),
                 )
             )
-        steps.append(functools.partial(ag_finish, part, 0))
+        steps.append(
+            functools.partial(
+                sequence, functools.partial(ag_finish, part, 0), lambda: put(part).start()
+            )
+        )
         return steps
 
-    part_a, part_b, part_c = (part_steps(part) for part in range(3))
+    def put(part):
+        off, n = plan.parts[part]
+        rows = slice(off, off + n)
+        return pltpu.make_async_copy(red_ref.at[rows], red_hbm.at[rows], out_sem.at[part])
+
+    all_steps = [part_steps(part) for part in range(len(plan.parts))]
+
+    def step(part, number):
+        all_steps[part][number]()
 
     load_o.wait()
     load_up.wait()
@@ -534,7 +521,7 @@
 
     def feed(t, carry):
         w2_rows = pl.ds(pl.multiple_of(t * tile, tile), tile)
-        pre = dot(second[...], w1[t]) + inb_ref[pl.ds(t, 1), :]
+        pre = dot(second[...], w1[t]) + inb[pl.ds(t, 1), :]
         square = pre * pre
         bend = jnp.tanh(curve * (pre + 0.044715 * (square * pre)))
         half = 0.5 * (1.0 + bend)
@@ -543,15 +530,18 @@
         upstream = up[...]
         racc[...] += dot(act, w2[w2_rows])
         d_pre = (dot_nt(upstream, w2[w2_rows]) * slope).astype(BF16)
-        base = (t // 2) * 4 * tile + (t % 2) * tile
+        base = 2 * t * tile
         grads[rows_at(base, tile)] = dot_tn(act, upstream).astype(BF16)
-        grads[rows_at(base + 2 * tile, tile)] = dot_tn(second[...], d_pre).astype(BF16)
+        grads[rows_at(base + tile, tile)] = dot_tn(second[...], d_pre).astype(BF16)
+        rs_start(t, 0)
         vstage[0, pl.ds(V_INNB + t, 1), :] = total(d_pre.astype(F32))
         dsec[...] += dot_nt(d_pre, w1[t])
 
-        @pl.when(t == 1)
-        def _():
-            part_a[0]()
+        for when in range(2, tiles):
+
+            @pl.when(t == when)
+            def _():
+                step(when - 2, 1)
 
         return carry
 
@@ -569,17 +559,16 @@
     d_branch = d_mid.astype(BF16)
     vstage[0, V_OB : V_OB + 1] = total(d_branch.astype(F32))
     grads[2 * hidden : 2 * hidden + width] = dot_tn(att[...], d_branch).astype(BF16)
-    part_b[0]()
     d_att = dot_nt(d_branch, wo[...]).astype(BF16)
     for b in range(pairs):
         dah[b] = d_att[:, b * LANES : (b + 1) * LANES]
 
+    step(tiles - 2, 1)
     schedule = {
-        0: [part_a[1]],
-        1: [part_b[1]],
-        3: [part_a[2]],
-        5: [part_b[2], part_a[3]],
-        7: [part_a[4], part_b[3]],
+        0: [(tiles - 1, 1)],
+        2: [(0, 2)],
+        4: [(1, 2)],
+        6: [(2, 2)],
     }
 
     def attend_back(i, carry):
@@ -599,11 +588,13 @@
 
             @pl.when(i == when)
             def _():
-                sequence(*steps)
+                for item in steps:
+                    step(*item)
 
         return carry
 
     lax.fori_loop(0, plan.chunks * pairs, attend_back, 0)
+    step(3, 2)
 
     def fold(b, carry):
         for c in range(plan.chunks):
@@ -661,13 +652,13 @@
 
     d_query = dq[...]
     vstage[0, V_QB : V_QB + 1] = total(d_query.astype(F32))
-    off_c = plan.parts[2][0]
+    off_c = 2 * hidden + width
     grads[off_c : off_c + width] = dot_tn(first[...], d_query).astype(BF16)
     d_first = dot_nt(d_query, wq[...])
     racc[...] = d_first
-    sequence(part_b[4], part_a[5])
-
-    spread = averaging(1)
+    step(4, 0)
+    step(0, 3)
+
     halo_wait(hsend, hrecv, back_send, back_recv)
     for k in range(1, seq):
         far_back(k).wait()
@@ -684,7 +675,7 @@
         coarse[:far_at, cols] = own[b, span : span + far_at].astype(BF16)
         coarse[far_at:, cols] = far_sum[b].astype(BF16)
     for half in range(2):
-        passed = dot(spread, coarse[:, half * width : (half + 1) * width])
+        passed = dot(spread[...], coarse[:, half * width : (half + 1) * width])
         for b in range(pairs):
             cols = slice((half * pairs + b) * LANES, (half * pairs + b + 1) * LANES)
             dkv[:, cols] = (
@@ -694,8 +685,10 @@
     vstage[0, V_VB : V_VB + 1] = total(d_values.astype(F32))
     grads[off_c + width : off_c + 2 * width] = dot_tn(first[...], d_keys).astype(BF16)
     grads[off_c + 2 * width : off_c + 3 * width] = dot_tn(first[...], d_values).astype(BF16)
-    part_c[0]()
-
+    step(5, 0)
+    step(1, 3)
+    step(4, 1)
+    step(2, 3)
     d_first = racc[...] + dot_nt(d_keys, wk[...]) + dot_nt(d_values, wv[...])
     normed = n1[...]
     scaled = d_first * vec(0)
@@ -729,68 +722,65 @@
             vstage[digit + 1] = acc
 
     vec_start(0)
-
-    part_c[1]()
-    part_b[5]()
-    vec_finish(0)
-    vec_start(1)
-    part_a[6]()
-    part_c[2]()
-    vec_finish(1)
-    vec_start(2)
-    part_b[6]()
-    part_c[3]()
-    vec_finish(2)
-    vec_start(3)
-    part_a[7]()
-    part_c[4]()
-    part_b[7]()
-    part_c[5]()
-    part_c[6]()
-    vec_finish(3)
-    part_a[8]()
-    part_c[7]()
-    part_b[8]()
-    part_c[8]()
-
-    for part in range(3):
+    tail = [
+        (3, 3), (0, 4), (1, 4), "v0", (4, 2), (5, 1), (2, 4), "v1", (4, 3), (3, 4), (5, 2), (0, 5),
+        "v2", (5, 3), (1, 5), (0, 6), (2, 5), "v3", (1, 6), (4, 4), (0, 7), (2, 6), (0, 8), (3, 5),
+        (1, 7), (5, 4), (1, 8), (2, 7), (4, 5), (3, 6), (2, 8), (5, 5), (4, 6), (3, 7), (5, 6),
+        (3, 8), (4, 7), (5, 7), (4, 8), (5, 8),
+    ]
+    for item in tail:
+        if isinstance(item, str):
+            digit = int(item[1])
+            vec_finish(digit)
+            if digit < 3:
+                vec_start(digit + 1)
+        else:
+            step(*item)
+
+    for part in range(len(plan.parts)):
         for digit in range(4):
             for k in range(1, count[digit]):
                 rs_copy(part, digit, k).wait_send()
-                if digit < 3 or plan.scatter[part]:
+                if digit < 3 or plan.scatter:
                     ag_copy(part, digit, k).wait_send()
+        put(part).wait()
     for digit in range(4):
         for k in range(1, count[digit]):
             vec_copy(digit, k).wait_send()
 
 
 def unpack_kernel(
-    width, tiles, red_hbm, vec_ref,
+    width, tiles, red_hbm, vec_ref, out_hbm, gin_hbm,
     query_ref, key_ref, value_ref, output_ref, inner_ref, outer_ref,
     preg_ref, pres_ref, qb_ref, vb_ref, ob_ref, midg_ref, mids_ref, outb_ref, innb_ref,
-    low, wide, in_sem, out_sem,
+    out_ref, gin_ref, low, wide, through, in_sem, out_sem, through_in, through_out,
 ):
     targets = []
     for t in range(tiles):
-        at = (t // 2) * 4 + t % 2
         rows = slice(t * width, (t + 1) * width)
-        targets.append((at, outer_ref.at[rows]))
-        targets.append((at + 2, inner_ref.at[:, rows]))
-    for i, ref in enumerate((output_ref, query_ref, key_ref, value_ref)):
-        targets.append((2 * tiles + i, ref))
+        targets.append(outer_ref.at[rows])
+        targets.append(inner_ref.at[:, rows])
+    targets += [output_ref, query_ref, key_ref, value_ref]
 
     def fetch(i):
-        at = targets[i][0]
         return pltpu.make_async_copy(
-            red_hbm.at[at * width : (at + 1) * width], low.at[i % 4], in_sem.at[i % 4]
+            red_hbm.at[i * width : (i + 1) * width], low.at[i % 4], in_sem.at[i % 4]
         )
 
     def put(i):
-        return pltpu.make_async_copy(wide.at[i % 4], targets[i][1], out_sem.at[i % 4])
+        return pltpu.make_async_copy(wide.at[i % 4], targets[i], out_sem.at[i % 4])
+
+    def take(i):
+        return pltpu.make_async_copy((out_hbm, gin_hbm)[i], through.at[i], through_in.at[i])
+
+    def give(i):
+        return pltpu.make_async_copy(through.at[i], (out_ref, gin_ref)[i], through_out.at[i])
 
     n = len(targets)
-    for i in range(min(3, n)):
+    for i in range(3):
         fetch(i).start()
+    for i in range(2):
+        take(i).start()
     for row, ref in (
         (V_PREG, preg_ref), (V_PRES, pres_ref), (V_QB, qb_ref), (V_VB, vb_ref), (V_OB, ob_ref),
         (V_MIDG, midg_ref), (V_MIDS, mids_ref), (V_OUTB, outb_ref),
@@ -806,8 +796,13 @@
         put(i).start()
         if i + 3 < n:
             fetch(i + 3).start()
-    for i in range(max(0, n - 4), n):
+        if 2 <= i < 4:
+            take(i - 2).wait()
+            give(i - 2).start()
+    for i in range(n - 4, n):
         put(i).wait()
+    for i in range(2):
+        give(i).wait()
 
 
 def shards(
@@ -821,21 +816,16 @@
     plan = Plan(rows, seq, span, width, hidden)
     tiles = hidden // width
     pairs = width // LANES
-    vectors = jnp.concatenate(
-        [
-            prenorm_gain, prenorm_shift, query_bias, value_bias, output_bias, midnorm_gain,
-            midnorm_shift, outer_bias,
-        ]
-    ).reshape(8, width)
     count = plan.counts
     most = max(count) - 1
     vmem = pl.BlockSpec(memory_space=pltpu.VMEM)
     hbm = pl.BlockSpec(memory_space=pl.ANY)
     grad_rows = plan.grad_rows
     rest = [grad_rows // 2, grad_rows // 4, grad_rows // 4 // count[2]]
-    last = rest[2] // seq if all(plan.scatter) else rest[2]
+    last = rest[2] // seq if plan.scatter else rest[2]
     dma = pltpu.SemaphoreType.DMA
     items = plan.chunks * pairs
+    n_parts = len(plan.parts)
     scratch = [
         pltpu.VMEM((span, width), BF16),
         pltpu.VMEM((span, width), BF16),
@@ -856,12 +846,11 @@
         pltpu.VMEM((span, width), BF16),
         pltpu.VMEM((pairs, span, LANES), BF16),
         pltpu.VMEM((span, width), BF16),
-        pltpu.VMEM((2 * pairs, span + plan.far_row, LANES), BF16),
-        pltpu.VMEM((2, 2 * pairs, plan.edge, LANES), BF16),
-        pltpu.VMEM((2, 2 * pairs, plan.edge, LANES), BF16),
-        pltpu.VMEM((seq, NR, 2 * width), BF16),
-        pltpu.VMEM((plan.chunks, 2 * pairs, plan.slots, LANES), BF16),
-        pltpu.VMEM((seq, 8, span), BF16),
+        pltpu.VMEM((2 * pairs + 1, span + plan.far_row, LANES), BF16),
+        pltpu.VMEM((2, 2 * pairs + 1, plan.edge, LANES), BF16),
+        pltpu.VMEM((2, 2 * pairs + 1, plan.edge, LANES), BF16),
+        pltpu.VMEM((seq, NR, 2 * width + LANES), BF16),
+        pltpu.VMEM((plan.chunks, 2 * pairs + 1, plan.slots, LANES), BF16),
         pltpu.VMEM((plan.chunks, plan.chunk, plan.slots), F32),
         pltpu.VMEM((items, 2 * plan.chunk, plan.slots), BF16),
         pltpu.VMEM((plan.chunks, 2 * pairs, plan.slots, LANES), F32),
@@ -871,6 +860,7 @@
         pltpu.VMEM((seq, 2 * pairs, NR, LANES), BF16),
         pltpu.VMEM((seq - 1, 2 * pairs, NR, LANES), BF16),
         pltpu.VMEM((plan.coarse_rows, 2 * width), BF16),
+        pltpu.VMEM((span, plan.coarse_rows), BF16),
         pltpu.VMEM((span, 2 * width), BF16),
         pltpu.VMEM((grad_rows, width), BF16),
         pltpu.VMEM((count[0] - 1, rest[0], width), BF16),
@@ -883,13 +873,16 @@
         pltpu.VMEM((count[2], VEC_ROWS, width), F32),
         pltpu.VMEM((count[3], VEC_ROWS, width), F32),
         pltpu.VMEM((2, span, LANES), F32),
+        pltpu.VMEM((tiles, width), F32),
+        pltpu.VMEM((grad_rows, width), BF16),
         dma((7 + tiles,)),
+        dma((n_parts,)),
         dma((2,)), dma((2,)),
         dma((seq - 1,)), dma((seq - 1,)),
         dma((2,)), dma((2,)),
         dma((seq - 1,)), dma((seq - 1,)),
-        dma((3, 4, most)), dma((3, 4, most)),
-        dma((3, 4, most)), dma((3, 4, most)),
+        dma((n_parts, 4, most)), dma((n_parts, 4, most)),
+        dma((n_parts, 4, most)), dma((n_parts, 4, most)),
         dma((4, most)), dma((4, most)),
     ]
     layer_output, input_grad, reduced, vecs = pl.pallas_call(
@@ -900,16 +893,20 @@
             jax.ShapeDtypeStruct((grad_rows, width), BF16),
             jax.ShapeDtypeStruct((VEC_ROWS, width), F32),
         ),
-        in_specs=[hbm, vmem, vmem, vmem] + [hbm] * 7,
-        out_specs=(vmem, vmem, vmem, vmem),
+        in_specs=[
+            hbm, vmem, vmem, vmem, hbm, vmem, hbm, hbm, vmem, hbm, vmem, vmem, vmem, hbm, vmem, hbm,
+            vmem, hbm,
+        ],
+        out_specs=(vmem, vmem, hbm, vmem),
         scratch_shapes=scratch,
         compiler_params=pltpu.CompilerParams(
             collective_id=0, has_side_effects=True, vmem_limit_bytes=60 * 1024 * 1024
         ),
         name="layer",
     )(
-        tokens, segment_ids, vectors, inner_bias.reshape(tiles, width), query_proj, key_proj,
-        value_proj, output_proj, inner_proj, outer_proj, upstream,
+        tokens, segment_ids, prenorm_gain, prenorm_shift, query_proj, query_bias, key_proj,
+        value_proj, value_bias, output_proj, output_bias, midnorm_gain, midnorm_shift, inner_proj,
+        inner_bias, outer_proj, outer_bias, upstream,
     )
     matrix = jax.ShapeDtypeStruct((width, width), F32)
     vector = jax.ShapeDtypeStruct((width,), F32)
@@ -921,18 +918,21 @@
             jax.ShapeDtypeStruct((hidden, width), F32),
             vector, vector, vector, vector, vector, vector, vector, vector,
             jax.ShapeDtypeStruct((hidden,), F32),
+            jax.ShapeDtypeStruct(tokens.shape, BF16),
+            jax.ShapeDtypeStruct(tokens.shape, BF16),
         ),
-        in_specs=[hbm, vmem],
-        out_specs=(hbm,) * 6 + (vmem,) * 9,
+        in_specs=[hbm, vmem, hbm, hbm],
+        out_specs=(hbm,) * 6 + (vmem,) * 9 + (hbm,) * 2,
         scratch_shapes=[
             pltpu.VMEM((4, width, width), BF16),
             pltpu.VMEM((4, width, width), F32),
-            dma((4,)), dma((4,)),
+            pltpu.VMEM((2, 1, span, width), BF16),
+            dma((4,)), dma((4,)), dma((2,)), dma((2,)),
         ],
         name="unpack",
-    )(reduced, vecs)
+    )(reduced, vecs, layer_output, input_grad)
     (query_g, key_g, value_g, output_g, inner_g, outer_g,
-     preg, pres, qb, vb, ob, midg, mids, outb, innb) = grads
+     preg, pres, qb, vb, ob, midg, mids, outb, innb, layer_output, input_grad) = grads
     return (
         layer_output, input_grad, preg, pres, query_g, qb, key_g, value_g, vb, output_g, ob,
         midg, mids, inner_g, innb, outer_g, outb,

time: 146 us -> 122 us (0.84)
  Pallas kernels: 134 us -> 119 us
  local copies, waits for them, and re-layouts: 8.82 us -> 0 us
    pallas_call x1, Pallas kernels: 125 us -> 110 us  [shards(): pl.pallas_call(functools.partial(layer_kernel, plan), out_shape=(jax.Shap...]
    unnamed x13 -> x0, local copies, waits for them, and re-layouts: 6.22 us -> none
    reshape x2 -> x0, local copies, waits for them, and re-layouts: 1.91 us -> none  [the longest x1 1.3 us: shards(): inner_bias.reshape(tiles, width)]
where the time goes in v2:
time: 122 us; the launch traced here: 120 us
  Pallas kernels  119 us (98%)
    pallas_call x1, Pallas kernels, shards(): pl.pallas_call(functools.partial(layer_kernel, plan), out_shape=(jax.Shap...  110 us
    pallas_call x1, Pallas kernels, shards(): pl.pallas_call(functools.partial(unpack_kernel, width, tiles), out_shape=...  9.29 us

profile of v2, /device:TPU:0, one launch (start us, length us, event | category | flops | bytes accessed | tf_op | source)
XLA Modules:
  0.0 120.0 jit_solution(4159246084639789063)
XLA Ops:
  0.7 110.1 %layer.1 = (bf16[1,256,512]{2,1,0:T(8,128)(2,1)}, bf16[1,256,512]{2,1,0:T(8,128)(2,1)}, bf16[6144,512]{1,0:T(8,128)(2,1)}, f32[16,512]{1,0:T(8,128)}) custom-call(bf16[1,256,512]{2,1,0:T(8,128)(2,1)} %tok_hbm.1, s32[1,256]{1,0:T(1,128)} %ids_ref.1, f32[512]{0:T(512)} %preg_ref.1, f32[512]{0:T(512)} %pres_ref.1, bf16[512,512]{1,0:T(8,128)(2,1)} %wq_hbm.1, ...), custom_call_target="tpu_custom_call" | custom-call | tf_op jit(solution)/shard_map/layer/pallas_call | solution.py:888
  110.7 9.3 %unpack.1 = (f32[512,512]{1,0:T(8,128)}, f32[512,512]{1,0:T(8,128)}, f32[512,512]{1,0:T(8,128)}, f32[512,512]{1,0:T(8,128)}, f32[512,2048]{1,0:T(8,128)}, /*inde...) custom-call(bf16[6144,512]{1,0:T(8,128)(2,1)} %get-tuple-element.38., ...), custom_call_target="tpu_custom_call" | custom-call | tf_op jit(solution)/shard_map/unpack/pallas_call | solution.py:913

commit v3 on v2

--- a/solution.py
+++ b/solution.py
@@ -45,6 +45,27 @@
 
 def total(x):
     return jnp.sum(x, axis=0, keepdims=True)
+
+
+ORDER = {
+    "f2": [0, 1],
+    "f3": [2, 3],
+    "ln2": [4],
+    "b0": [5],
+    "b1": [0, 6],
+    "b2": [1, 7, 8],
+    "b4": [2],
+    "b6": [0],
+    "b7": [3, 1],
+    "fold": [2],
+    "q": [4, 0, 3, 1, 5, 9, 4, 6, 5, 7],
+    "ln1": [
+        2, 6, 8, 0, 7, 10, 9, 11, 3, 8, 1, 0, 4, -1, 9, 10, 5, 1, 2, 11, 6, 10, 0, -1,
+        7, 2, 3, 0, 11, 1, 8, 4, 1, 2, 3, 9, -1, 4, 5, 2, 6, 3, 10, 5, 3, 7, 4, 6,
+        11, -1, 8, 4, 5, 7, 9, 6, 10, 8, 5, 11, 6, 9, 7, 10, 7, 11, 8, 9, 8, 10, 9, 11,
+        10, 11,
+    ],
+}
 
 
 class Plan:
@@ -79,10 +100,10 @@
         self.far_slots = self.slots - self.far_slot
         self.edge = NR * (self.near + 1)
         self.grad_rows = 4 * width + 2 * hidden
-        self.parts = [(p * 2 * width, 2 * width) for p in range(self.grad_rows // (2 * width))]
+        self.parts = [(p * width, width) for p in range(self.grad_rows // width)]
         self.counts = [2, 2, rows // 4, seq]
         self.swap = rows // 4 == 2
-        self.scatter = (2 * width // rows) % (NR * seq) == 0
+        self.scatter = (width // rows) % (NR * seq) == 0
 
 
 def sequence(*steps):
@@ -502,6 +523,23 @@
     def step(part, number):
         all_steps[part][number]()
 
+    at_place = {}
+    reached_step = [0] * (len(plan.parts) + 1)
+    for place, parts_here in ORDER.items():
+        at_place[place] = []
+        for part in parts_here:
+            reached_step[part] += 1
+            at_place[place].append((part, reached_step[part]))
+
+    def advance(place):
+        for part, number in at_place.get(place, ()):
+            if part < 0:
+                vec_finish(number - 1)
+                if number < 4:
+                    vec_start(number)
+            else:
+                step(part, number)
+
     load_o.wait()
     load_up.wait()
     res = tok[...].astype(F32) + dot(att[...], wo[...]) + vec(4)
@@ -533,15 +571,14 @@
         base = 2 * t * tile
         grads[rows_at(base, tile)] = dot_tn(act, upstream).astype(BF16)
         grads[rows_at(base + tile, tile)] = dot_tn(second[...], d_pre).astype(BF16)
-        rs_start(t, 0)
+        rs_start(2 * t, 0)
+        rs_start(2 * t + 1, 0)
         vstage[0, pl.ds(V_INNB + t, 1), :] = total(d_pre.astype(F32))
         dsec[...] += dot_nt(d_pre, w1[t])
 
-        for when in range(2, tiles):
-
-            @pl.when(t == when)
-            def _():
-                step(when - 2, 1)
+        for when in range(tiles):
+            if f"f{when}" in ORDER:
+                pl.when(t == when)(functools.partial(advance, f"f{when}"))
 
         return carry
 
@@ -559,17 +596,11 @@
     d_branch = d_mid.astype(BF16)
     vstage[0, V_OB : V_OB + 1] = total(d_branch.astype(F32))
     grads[2 * hidden : 2 * hidden + width] = dot_tn(att[...], d_branch).astype(BF16)
+    rs_start(2 * tiles, 0)
+    advance("ln2")
     d_att = dot_nt(d_branch, wo[...]).astype(BF16)
     for b in range(pairs):
         dah[b] = d_att[:, b * LANES : (b + 1) * LANES]
-
-    step(tiles - 2, 1)
-    schedule = {
-        0: [(tiles - 1, 1)],
-        2: [(0, 2)],
-        4: [(1, 2)],
-        6: [(2, 2)],
-    }
 
     def attend_back(i, carry):
         c, b = i // pairs, i % pairs
@@ -584,17 +615,13 @@
         dq[chunk_rows(c), pair_lanes(b)] = d_query.astype(BF16)
         dslots[c, b] = dot_tn(d_score, q2)
         dslots[c, pairs + b] = dot_tn(low, g2)
-        for when, steps in schedule.items():
-
-            @pl.when(i == when)
-            def _():
-                for item in steps:
-                    step(*item)
+        for when in range(plan.chunks * pairs):
+            if f"b{when}" in ORDER:
+                pl.when(i == when)(functools.partial(advance, f"b{when}"))
 
         return carry
 
     lax.fori_loop(0, plan.chunks * pairs, attend_back, 0)
-    step(3, 2)
 
     def fold(b, carry):
         for c in range(plan.chunks):
@@ -650,14 +677,16 @@
     for k in range(1, seq):
         far_back(k).start()
 
+    advance("fold")
+
     d_query = dq[...]
     vstage[0, V_QB : V_QB + 1] = total(d_query.astype(F32))
     off_c = 2 * hidden + width
     grads[off_c : off_c + width] = dot_tn(first[...], d_query).astype(BF16)
     d_first = dot_nt(d_query, wq[...])
     racc[...] = d_first
-    step(4, 0)
-    step(0, 3)
+    rs_start(2 * tiles + 1, 0)
+    advance("q")
 
     halo_wait(hsend, hrecv, back_send, back_recv)
     for k in range(1, seq):
@@ -685,10 +714,9 @@
     vstage[0, V_VB : V_VB + 1] = total(d_values.astype(F32))
     grads[off_c + width : off_c + 2 * width] = dot_tn(first[...], d_keys).astype(BF16)
     grads[off_c + 2 * width : off_c + 3 * width] = dot_tn(first[...], d_values).astype(BF16)
-    step(5, 0)
-    step(1, 3)
-    step(4, 1)
-    step(2, 3)
+    rs_start(2 * tiles + 2, 0)
+    rs_start(2 * tiles + 3, 0)
+    advance("dkv")
     d_first = racc[...] + dot_nt(d_keys, wk[...]) + dot_nt(d_values, wv[...])
     normed = n1[...]
     scaled = d_first * vec(0)
@@ -722,20 +750,7 @@
             vstage[digit + 1] = acc
 
     vec_start(0)
-    tail = [
-        (3, 3), (0, 4), (1, 4), "v0", (4, 2), (5, 1), (2, 4), "v1", (4, 3), (3, 4), (5, 2), (0, 5),
-        "v2", (5, 3), (1, 5), (0, 6), (2, 5), "v3", (1, 6), (4, 4), (0, 7), (2, 6), (0, 8), (3, 5),
-        (1, 7), (5, 4), (1, 8), (2, 7), (4, 5), (3, 6), (2, 8), (5, 5), (4, 6), (3, 7), (5, 6),
-        (3, 8), (4, 7), (5, 7), (4, 8), (5, 8),
-    ]
-    for item in tail:
-        if isinstance(item, str):
-            digit = int(item[1])
-            vec_finish(digit)
-            if digit < 3:
-                vec_start(digit + 1)
-        else:
-            step(*item)
+    advance("ln1")
 
     for part in range(len(plan.parts)):
         for digit in range(4):

time: 122 us -> 108 us (0.89); the launches traced: 120 us -> 107 us
  Pallas kernels: 119 us -> 107 us
    pallas_call x1, Pallas kernels: 110 us -> 97.3 us  [shards(): pl.pallas_call(functools.partial(layer_kernel, plan), out_shape=(jax.Shap...]
where the time goes in v3:
time: 108 us; the launch traced here: 107 us
  Pallas kernels  107 us (99%)
    pallas_call x1, Pallas kernels, shards(): pl.pallas_call(functools.partial(layer_kernel, plan), out_shape=(jax.Shap...  97.3 us
    pallas_call x1, Pallas kernels, shards(): pl.pallas_call(functools.partial(unpack_kernel, width, tiles), out_shape=...  9.29 us

profile of v3, /device:TPU:0, one launch (start us, length us, event | category | flops | bytes accessed | tf_op | source)
XLA Modules:
  0.0 107.3 jit_solution(2168212792006942579)
XLA Ops:
  0.7 97.3 %layer.1 = (bf16[1,256,512]{2,1,0:T(8,128)(2,1)}, bf16[1,256,512]{2,1,0:T(8,128)(2,1)}, bf16[6144,512]{1,0:T(8,128)(2,1)}, f32[16,512]{1,0:T(8,128)}) custom-call(bf16[1,256,512]{2,1,0:T(8,128)(2,1)} %tok_hbm.1, s32[1,256]{1,0:T(1,128)} %ids_ref.1, f32[512]{0:T(512)} %preg_ref.1, f32[512]{0:T(512)} %pres_ref.1, bf16[512,512]{1,0:T(8,128)(2,1)} %wq_hbm.1, ...), custom_call_target="tpu_custom_call" | custom-call | tf_op jit(solution)/shard_map/layer/pallas_call | solution.py:903
  98.0 9.3 %unpack.1 = (f32[512,512]{1,0:T(8,128)}, f32[512,512]{1,0:T(8,128)}, f32[512,512]{1,0:T(8,128)}, f32[512,512]{1,0:T(8,128)}, f32[512,2048]{1,0:T(8,128)}, /*inde...) custom-call(bf16[6144,512]{1,0:T(8,128)(2,1)} %get-tuple-element.38., ...), custom_call_target="tpu_custom_call" | custom-call | tf_op jit(solution)/shard_map/unpack/pallas_call | solution.py:928

commit v4 on v3

--- a/solution.py
+++ b/solution.py
@@ -115,12 +115,12 @@
     plan,
     tok_hbm, ids_ref, preg_ref, pres_ref, wq_hbm, qb_ref, wk_hbm, wv_hbm, vb_ref, wo_hbm, ob_ref,
     midg_ref, mids_ref, w1_hbm, inb_ref, w2_hbm, outb_ref, up_hbm,
-    out_ref, gin_ref, red_hbm, vout_ref,
+    out_ref, gin_ref, red_ref, vout_ref,
     tok, up, wq, wk, wv, wo, w1, w2, n1, n2, mid, racc, dsec, first, second, qh, att, dah, dq,
     level, edge, halo, farg, slots, bias, probs, dslots, own, hsend, hrecv, fsend, frecv,
     coarse, spread, dkv, grads, recv0, recv1, recv2, recv3, vstage, vrecv0, vrecv1, vrecv2, vrecv3, stats,
-    inb, red_ref,
-    in_sem, out_sem, halo_send, halo_recv, far_send, far_recv, back_send, back_recv, fback_send, fback_recv,
+    inb,
+    in_sem, halo_send, halo_recv, far_send, far_recv, back_send, back_recv, fback_send, fback_recv,
     rs_send, rs_recv, ag_send, ag_recv, vec_send, vec_recv,
 ):
     span, width, hidden = plan.span, plan.width, plan.hidden
@@ -506,17 +506,8 @@
                     functools.partial(ag_start, part, digit),
                 )
             )
-        steps.append(
-            functools.partial(
-                sequence, functools.partial(ag_finish, part, 0), lambda: put(part).start()
-            )
-        )
+        steps.append(functools.partial(ag_finish, part, 0))
         return steps
-
-    def put(part):
-        off, n = plan.parts[part]
-        rows = slice(off, off + n)
-        return pltpu.make_async_copy(red_ref.at[rows], red_hbm.at[rows], out_sem.at[part])
 
     all_steps = [part_steps(part) for part in range(len(plan.parts))]
 
@@ -758,17 +749,16 @@
                 rs_copy(part, digit, k).wait_send()
                 if digit < 3 or plan.scatter:
                     ag_copy(part, digit, k).wait_send()
-        put(part).wait()
     for digit in range(4):
         for k in range(1, count[digit]):
             vec_copy(digit, k).wait_send()
 
 
 def unpack_kernel(
-    width, tiles, red_hbm, vec_ref, out_hbm, gin_hbm,
+    width, tiles, red_ref, vec_ref, out_in, gin_in,
     query_ref, key_ref, value_ref, output_ref, inner_ref, outer_ref,
     preg_ref, pres_ref, qb_ref, vb_ref, ob_ref, midg_ref, mids_ref, outb_ref, innb_ref,
-    out_ref, gin_ref, low, wide, through, in_sem, out_sem, through_in, through_out,
+    out_ref, gin_ref, wide, out_sem, through_sem,
 ):
     targets = []
     for t in range(tiles):
@@ -777,25 +767,19 @@
         targets.append(inner_ref.at[:, rows])
     targets += [output_ref, query_ref, key_ref, value_ref]
 
-    def fetch(i):
+    def put(i):
+        return pltpu.make_async_copy(wide.at[i], targets[i], out_sem.at[i])
+
+    def give(i):
         return pltpu.make_async_copy(
-            red_hbm.at[i * width : (i + 1) * width], low.at[i % 4], in_sem.at[i % 4]
+            (out_in, gin_in)[i], (out_ref, gin_ref)[i], through_sem.at[i]
         )
 
-    def put(i):
-        return pltpu.make_async_copy(wide.at[i % 4], targets[i], out_sem.at[i % 4])
-
-    def take(i):
-        return pltpu.make_async_copy((out_hbm, gin_hbm)[i], through.at[i], through_in.at[i])
-
-    def give(i):
-        return pltpu.make_async_copy(through.at[i], (out_ref, gin_ref)[i], through_out.at[i])
-
-    n = len(targets)
-    for i in range(3):
-        fetch(i).start()
     for i in range(2):
-        take(i).start()
+        give(i).start()
+    for i in range(len(targets)):
+        wide[i] = red_ref[i * width : (i + 1) * width].astype(F32)
+        put(i).start()
     for row, ref in (
         (V_PREG, preg_ref), (V_PRES, pres_ref), (V_QB, qb_ref), (V_VB, vb_ref), (V_OB, ob_ref),
         (V_MIDG, midg_ref), (V_MIDS, mids_ref), (V_OUTB, outb_ref),
@@ -803,18 +787,7 @@
         ref[...] = vec_ref[row]
     for t in range(tiles):
         innb_ref[t * width : (t + 1) * width] = vec_ref[V_INNB + t]
-    for i in range(n):
-        fetch(i).wait()
-        if i >= 4:
-            put(i - 4).wait()
-        wide[i % 4] = low[i % 4].astype(F32)
-        put(i).start()
-        if i + 3 < n:
-            fetch(i + 3).start()
-        if 2 <= i < 4:
-            take(i - 2).wait()
-            give(i - 2).start()
-    for i in range(n - 4, n):
+    for i in range(len(targets)):
         put(i).wait()
     for i in range(2):
         give(i).wait()
@@ -889,9 +862,7 @@
         pltpu.VMEM((count[3], VEC_ROWS, width), F32),
         pltpu.VMEM((2, span, LANES), F32),
         pltpu.VMEM((tiles, width), F32),
-        pltpu.VMEM((grad_rows, width), BF16),
         dma((7 + tiles,)),
-        dma((n_parts,)),
         dma((2,)), dma((2,)),
         dma((seq - 1,)), dma((seq - 1,)),
         dma((2,)), dma((2,)),
@@ -903,19 +874,19 @@
     layer_output, input_grad, reduced, vecs = pl.pallas_call(
         functools.partial(layer_kernel, plan),
         out_shape=(
-            jax.ShapeDtypeStruct(tokens.shape, BF16),
-            jax.ShapeDtypeStruct(tokens.shape, BF16),
-            jax.ShapeDtypeStruct((grad_rows, width), BF16),
-            jax.ShapeDtypeStruct((VEC_ROWS, width), F32),
+            pltpu.VMEM(tokens.shape, BF16),
+            pltpu.VMEM(tokens.shape, BF16),
+            pltpu.VMEM((grad_rows, width), BF16),
+            pltpu.VMEM((VEC_ROWS, width), F32),
         ),
         in_specs=[
             hbm, vmem, vmem, vmem, hbm, vmem, hbm, hbm, vmem, hbm, vmem, vmem, vmem, hbm, vmem, hbm,
             vmem, hbm,
         ],
-        out_specs=(vmem, vmem, hbm, vmem),
+        out_specs=(vmem, vmem, vmem, vmem),
         scratch_shapes=scratch,
         compiler_params=pltpu.CompilerParams(
-            collective_id=0, has_side_effects=True, vmem_limit_bytes=60 * 1024 * 1024
+            collective_id=0, has_side_effects=True, vmem_limit_bytes=50 * 1024 * 1024
         ),
         name="layer",
     )(
@@ -936,14 +907,13 @@
             jax.ShapeDtypeStruct(tokens.shape, BF16),
             jax.ShapeDtypeStruct(tokens.shape, BF16),
         ),
-        in_specs=[hbm, vmem, hbm, hbm],
+        in_specs=[vmem] * 4,
         out_specs=(hbm,) * 6 + (vmem,) * 9 + (hbm,) * 2,
         scratch_shapes=[
-            pltpu.VMEM((4, width, width), BF16),
-            pltpu.VMEM((4, width, width), F32),
-            pltpu.VMEM((2, 1, span, width), BF16),
-            dma((4,)), dma((4,)), dma((2,)), dma((2,)),
+            pltpu.VMEM((n_parts, width, width), F32),
+            dma((n_parts,)), dma((2,)),
         ],
+        compiler_params=pltpu.CompilerParams(vmem_limit_bytes=24 * 1024 * 1024),
         name="unpack",
     )(reduced, vecs, layer_output, input_grad)
     (query_g, key_g, value_g, output_g, inner_g, outer_g,

time: 108 us -> 102 us (0.944)
  Pallas kernels: 107 us -> 101 us
    pallas_call x1, Pallas kernels: 9.29 us -> 5.55 us  [shards(): pl.pallas_call(functools.partial(unpack_kernel, width, tiles), out_shape=...]
    pallas_call x1, Pallas kernels: 97.3 us -> 95.9 us  [shards(): pl.pallas_call(functools.partial(layer_kernel, plan), out_shape=(pltpu.VM...]
where the time goes in v4:
time: 102 us
  Pallas kernels  101 us (99%)
    pallas_call x1, Pallas kernels, shards(): pl.pallas_call(functools.partial(layer_kernel, plan), out_shape=(pltpu.VM...  95.9 us
    pallas_call x1, Pallas kernels, shards(): pl.pallas_call(functools.partial(unpack_kernel, width, tiles), out_shape=...  5.55 us

profile of v4, /device:TPU:0, one launch (start us, length us, event | category | flops | bytes accessed | tf_op | source)
XLA Modules:
  0.0 102.1 jit_solution(17808033633255206997)
XLA Ops:
  0.7 95.9 %layer.1 = (bf16[1,256,512]{2,1,0:T(8,128)(2,1)S(1)}, bf16[1,256,512]{2,1,0:T(8,128)(2,1)S(1)}, bf16[6144,512]{1,0:T(8,128)(2,1)S(1)}, f32[16,512]{1,0:T(8,128)S(1)}) custom-call(bf16[1,256,512]{2,1,0:T(8,128)(2,1)} %tok_hbm.1, s32[1,256]{1,0:T(1,128)} %ids_ref.1, f32[512]{0:T(512)} %preg_ref.1, f32[512]{0:T(512)} %pres_ref.1, bf16[512,512]{1,0:T(8,128)(2,1)} %wq_hbm.1, ...), custom_call_target="tpu_custom_call" | custom-call | tf_op jit(solution)/shard_map/layer/pallas_call | solution.py:874
  96.5 5.5 %unpack.1 = (f32[512,512]{1,0:T(8,128)}, f32[512,512]{1,0:T(8,128)}, f32[512,512]{1,0:T(8,128)}, f32[512,512]{1,0:T(8,128)}, f32[512,2048]{1,0:T(8,128)}, /*inde...) custom-call(bf16[6144,512]{1,0:T(8,128)(2,1)S(1)} %get-tuple-element, ...), custom_call_target="tpu_custom_call" | custom-call | tf_op jit(solution)/shard_map/unpack/pallas_call | solution.py:899

commit v5 on v4

--- a/solution.py
+++ b/solution.py
@@ -86,6 +86,7 @@
         for level in self.far:
             self.level_row.append(at)
             at += span >> level
+        self.far_rows = -(-(at - self.far_row) // 8) * 8
         self.coarse_rows = self.far_row + NR
         self.slot, self.slot_len = [], []
         at = 0
@@ -117,7 +118,7 @@
     midg_ref, mids_ref, w1_hbm, inb_ref, w2_hbm, outb_ref, up_hbm,
     out_ref, gin_ref, red_ref, vout_ref,
     tok, up, wq, wk, wv, wo, w1, w2, n1, n2, mid, racc, dsec, first, second, qh, att, dah, dq,
-    level, edge, halo, farg, slots, bias, probs, dslots, own, hsend, hrecv, fsend, frecv,
+    level, edge, halo, far_k, far_v, slots, bias, probs, dslots, own, hsend, hrecv, fsend, frecv,
     coarse, spread, dkv, grads, recv0, recv1, recv2, recv3, vstage, vrecv0, vrecv1, vrecv2, vrecv3, stats,
     inb,
     in_sem, halo_send, halo_recv, far_send, far_recv, back_send, back_recv, fback_send, fback_recv,
@@ -129,6 +130,8 @@
     tiles = w1.shape[0]
     pairs = width // LANES
     blocks = 2 * pairs
+    id_at, value_at = pairs, pairs + 1
+    far_rows = plan.far_rows
     row_id, seq_id = lax.axis_index("rows"), lax.axis_index("seq")
     start = seq_id * span
 
@@ -177,6 +180,9 @@
 
     halo[...] = jnp.zeros_like(halo)
     hrecv[...] = jnp.zeros_like(hrecv)
+    far_k[...] = jnp.zeros_like(far_k)
+    far_v[...] = jnp.zeros_like(far_v)
+    frecv[...] = jnp.zeros_like(frecv)
     vstage[0] = jnp.zeros((VEC_ROWS, width), F32)
     for t in range(tiles):
         inb[t : t + 1, :] = inb_ref[t * tile : (t + 1) * tile].reshape(1, tile)
@@ -202,14 +208,6 @@
     n1[...] = normed
     stats[0] = jnp.broadcast_to(rstd, (span, LANES))
     first[...] = (normed * vec(0) + vec(1)).astype(BF16)
-    load_k.wait()
-    keys = dot(first[...], wk[...]).astype(BF16)
-    load_v.wait()
-    values = (dot(first[...], wv[...]) + vec(3)).astype(BF16)
-    for b in range(pairs):
-        level[b, :span] = keys[:, b * LANES : (b + 1) * LANES]
-        level[pairs + b, :span] = values[:, b * LANES : (b + 1) * LANES]
-
     def averaging(rows_dim):
         shape = (plan.coarse_rows, span) if rows_dim == 0 else (span, plan.coarse_rows)
         r, p = iota(shape, rows_dim), iota(shape, 1 - rows_dim)
@@ -220,72 +218,117 @@
             matrix = jnp.where(hit, 0.5**lv, matrix)
         return matrix.astype(BF16)
 
+    def level_start(lv):
+        return 0 if lv == 0 else span + plan.level_row[lv]
+
+    far_at = plan.far_row
+
+    def fill(at, fresh, coarser):
+        for b in range(fresh.shape[1] // LANES):
+            cols = slice(b * LANES, (b + 1) * LANES)
+            level[at + b, :span] = fresh[:, cols]
+            level[at + b, span : span + far_at] = coarser[:far_at, cols]
+
+    def cut_edges(first_block, last_block):
+        for lv in range(near + 1):
+            at, n = level_start(lv), span >> lv
+            to = slice(lv * NR, (lv + 1) * NR)
+            edge[0, first_block:last_block, to] = level[first_block:last_block, at : at + NR]
+            edge[1, first_block:last_block, to] = level[first_block:last_block, at + n - NR : at + n]
+
+    def apart(other):
+        return (other - seq_id > 1) | (other - seq_id < -1)
+
+    class Halo:
+        def __init__(self, src, dst, send, recv, blocks_sent=None):
+            self.sems = send, recv
+            self.src, self.dst, self.sent = src, dst, blocks_sent
+
+        def copy(self, from_side, to_side, recv_side, step):
+            send, recv = self.sems
+            src, dst = self.src.at[from_side], self.dst.at[to_side]
+            if self.sent is not None:
+                src, dst = (
+                    self.src.at[from_side, pl.ds(*self.sent)],
+                    self.dst.at[to_side, pl.ds(*self.sent)],
+                )
+            return remote(
+                src, dst, send.at[from_side], recv.at[recv_side], (row_id, seq_id + step)
+            )
+
+        def start(self):
+            @pl.when(seq_id > 0)
+            def _():
+                self.copy(0, 1, 1, -1).start()
+
+            @pl.when(seq_id < seq - 1)
+            def _():
+                self.copy(1, 0, 0, 1).start()
+
+        def wait(self):
+            @pl.when(seq_id > 0)
+            def _():
+                self.copy(0, 0, 0, -1).wait()
+
+            @pl.when(seq_id < seq - 1)
+            def _():
+                self.copy(1, 1, 1, 1).wait()
+
+    class Far:
+        def __init__(self, src, dst, send, recv):
+            self.src, self.dst, self.send, self.recv = src, dst, send, recv
+
+        def copy(self, k):
+            other, device = peer(3, k)
+            return remote(
+                self.src(other), self.dst(k), self.send.at[k - 1], self.recv.at[k - 1], device
+            )
+
+        def start(self):
+            for k in range(1, seq):
+                pl.when(apart(peer(3, k)[0]))(lambda: self.copy(k).start())
+
+        def wait(self):
+            for k in range(1, seq):
+                pl.when(apart(peer(3, seq - k)[0]))(lambda: self.copy(k).wait_recv())
+                pl.when(apart(peer(3, k)[0]))(lambda: self.copy(k).wait_send())
+
+    key_halo = Halo(edge, halo, halo_send.at[0], halo_recv.at[0], (0, value_at))
+    value_halo = Halo(edge, halo, halo_send.at[1], halo_recv.at[1], (value_at, pairs))
+    key_far = Far(
+        lambda other: far_k.at[seq_id], lambda k: far_k.at[seq_id], far_send.at[0], far_recv.at[0]
+    )
+    value_far = Far(
+        lambda other: far_v.at[seq_id], lambda k: far_v.at[seq_id], far_send.at[1], far_recv.at[1]
+    )
+
     matrix = averaging(0)
-    far_at = plan.far_row
+    load_k.wait()
+    keys = dot(first[...], wk[...]).astype(BF16)
+    mixed = dot(matrix, keys).astype(BF16)
+    fill(0, keys, mixed)
+    far_k[seq_id, :, :width] = mixed[far_at : far_at + far_rows]
     feature = (iota((LANES, span), 0) == ids_ref[...]).astype(F32).astype(BF16)
     unit = (iota((span, span), 0) == iota((span, span), 1)).astype(F32).astype(BF16)
     id_hot = dot_nt(unit, feature).astype(BF16)
-    level[blocks, :span] = id_hot
-    for half, kv in enumerate((keys, values)):
-        mixed = dot(matrix, kv).astype(BF16)
-        for b in range(pairs):
-            level[half * pairs + b, span : span + far_at] = mixed[
-                :far_at, b * LANES : (b + 1) * LANES
-            ]
-        farg[seq_id, :, half * width : (half + 1) * width] = mixed[far_at:]
     alike = dot(matrix, id_hot)
     alike = jnp.where((alike > 0.999) & (iota(alike.shape, 1) > 0), 1.0, 0.0).astype(BF16)
-    level[blocks, span : span + far_at] = alike[:far_at]
-    farg[seq_id, :, 2 * width :] = alike[far_at:]
-
-    def level_start(lv):
-        return 0 if lv == 0 else span + plan.level_row[lv]
-
-    for lv in range(near + 1):
-        at, n = level_start(lv), span >> lv
-        edge[0, :, lv * NR : (lv + 1) * NR] = level[:, at : at + NR]
-        edge[1, :, lv * NR : (lv + 1) * NR] = level[:, at + n - NR : at + n]
+    fill(id_at, id_hot, alike)
+    far_k[seq_id, :, width:] = alike[far_at : far_at + far_rows]
+    cut_edges(0, value_at)
 
     pl.semaphore_wait(barrier, greeted)
-
-    def far_copy(k):
-        _, device = peer(3, k)
-        return remote(
-            farg.at[seq_id], farg.at[seq_id], far_send.at[k - 1], far_recv.at[k - 1], device
-        )
-
-    def halo_copy(src, dst, send, recv, side):
-        step = 2 * side - 1
-        return remote(
-            src.at[side], dst.at[1 - side], send.at[side], recv.at[1 - side],
-            (row_id, seq_id + step),
-        )
-
-    def halo_start(src, dst, send, recv):
-        @pl.when(seq_id > 0)
-        def _():
-            halo_copy(src, dst, send, recv, 0).start()
-
-        @pl.when(seq_id < seq - 1)
-        def _():
-            halo_copy(src, dst, send, recv, 1).start()
-
-    def halo_wait(src, dst, send, recv):
-        @pl.when(seq_id > 0)
-        def _():
-            remote(
-                src.at[0], dst.at[0], send.at[0], recv.at[0], (row_id, seq_id - 1)
-            ).wait()
-
-        @pl.when(seq_id < seq - 1)
-        def _():
-            remote(
-                src.at[1], dst.at[1], send.at[1], recv.at[1], (row_id, seq_id + 1)
-            ).wait()
-
-    halo_start(edge, halo, halo_send, halo_recv)
-    for k in range(1, seq):
-        far_copy(k).start()
+    key_far.start()
+    key_halo.start()
+
+    load_v.wait()
+    values = (dot(first[...], wv[...]) + vec(3)).astype(BF16)
+    mixed = dot(matrix, values).astype(BF16)
+    fill(value_at, values, mixed)
+    far_v[seq_id] = mixed[far_at : far_at + far_rows]
+    cut_edges(value_at, value_at + pairs)
+    value_far.start()
+    value_halo.start()
 
     load_q.wait()
     query = ((dot(first[...], wq[...]) + vec(2)).astype(BF16) * (1.0 / math.sqrt(HEAD_DIM))).astype(
@@ -340,32 +383,39 @@
         for lv in plan.far:
             per_log = (span >> lv).bit_length() - 1
             first_row = plan.level_row[lv] - plan.far_row
-            j = (start // (NR << lv) - 1) * NR + iota((3 * NR, seq * NR), 0)
-            column = (j >> per_log) * NR + (j & ((1 << per_log) - 1)) + first_row
-            pieces.append((column == iota((3 * NR, seq * NR), 1)).astype(F32))
+            j = (start // (NR << lv) - 1) * NR + iota((3 * NR, seq * far_rows), 0)
+            column = (j >> per_log) * far_rows + (j & ((1 << per_log) - 1)) + first_row
+            pieces.append((column == iota((3 * NR, seq * far_rows), 1)).astype(F32))
         rest = plan.far_slots - 3 * NR * len(plan.far)
         if rest:
-            pieces.append(jnp.zeros((rest, seq * NR), F32))
+            pieces.append(jnp.zeros((rest, seq * far_rows), F32))
         return jnp.concatenate(pieces, axis=0).astype(BF16)
 
     select = far_select()
     spread[...] = averaging(1)
 
-    halo_wait(edge, halo, halo_send, halo_recv)
+    def fill_slots(first_block, n_blocks, far_values):
+        those = slice(first_block, first_block + n_blocks)
+        for c in range(plan.chunks):
+            for s0, kind, at, n in slot_pieces(c):
+                if kind == "own":
+                    slots[c, those, s0 : s0 + n] = level[those, at : at + n]
+                else:
+                    slots[c, those, s0 : s0 + n] = halo[
+                        0 if kind == "low" else 1, those, at : at + n
+                    ]
+            for b in range(n_blocks):
+                slots[c, first_block + b, plan.far_slot :] = far_values[
+                    :, b * LANES : (b + 1) * LANES
+                ]
+
+    key_halo.wait()
+    key_far.wait()
+    fill_slots(
+        0, value_at, dot(select, far_k[...].reshape(seq * far_rows, width + LANES)).astype(BF16)
+    )
     for c in range(plan.chunks):
-        for s0, kind, at, n in slot_pieces(c):
-            if kind == "own":
-                slots[c, :, s0 : s0 + n] = level[:, at : at + n]
-            else:
-                slots[c, :, s0 : s0 + n] = halo[0 if kind == "low" else 1, :, at : at + n]
-    for k in range(1, seq):
-        far_copy(k).wait()
-    far_values = dot(select, farg[...].reshape(seq * NR, 2 * width + LANES)).astype(BF16)
-    for c in range(plan.chunks):
-        for b in range(blocks + 1):
-            slots[c, b, plan.far_slot :] = far_values[:, b * LANES : (b + 1) * LANES]
-    for c in range(plan.chunks):
-        same = dot_nt(level[blocks, c * plan.chunk : (c + 1) * plan.chunk], slots[c, blocks])
+        same = dot_nt(level[id_at, c * plan.chunk : (c + 1) * plan.chunk], slots[c, id_at])
         bias[c] = jnp.where(same > 0.5, bias[c], MASKED)
 
     lane = iota((1, LANES), 1)
@@ -393,12 +443,24 @@
         peak = jnp.max(score, axis=1, keepdims=True)
         raised = jnp.exp(score - peak)
         prob = raised * (1.0 / jnp.sum(raised, axis=1, keepdims=True))
-        low = prob.astype(BF16)
-        probs[i] = low
-        att[chunk_rows(c), pair_lanes(b)] = merge_heads(dot(low, slots[c, pairs + b])).astype(BF16)
+        probs[i] = prob.astype(BF16)
         return carry
 
-    lax.fori_loop(0, plan.chunks * pairs, attend, 0)
+    lax.fori_loop(0, plan.chunks * pairs, attend, 0, unroll=2)
+
+    value_halo.wait()
+    value_far.wait()
+    fill_slots(
+        value_at, pairs, dot(select, far_v[...].reshape(seq * far_rows, width)).astype(BF16)
+    )
+
+    def mix(i, carry):
+        c, b = i // pairs, i % pairs
+        both = dot(probs[i], slots[c, value_at + b])
+        att[chunk_rows(c), pair_lanes(b)] = merge_heads(both).astype(BF16)
+        return carry
+
+    lax.fori_loop(0, plan.chunks * pairs, mix, 0, unroll=2)
 
     received = [recv0, recv1, recv2, recv3]
 
@@ -438,7 +500,7 @@
 
     def rs_finish(part, digit):
         for k in range(1, count[digit]):
-            rs_copy(part, digit, k).wait_recv()
+            rs_copy(part, digit, k).wait()
         gather_all = digit == 3 and not plan.scatter
         base, n = region(part, digit if gather_all else digit + 1)
         at = part * n
@@ -481,7 +543,7 @@
         if digit == 3 and not plan.scatter:
             return
         for k in range(1, count[digit]):
-            ag_copy(part, digit, k).wait_recv()
+            ag_copy(part, digit, k).wait()
 
     def part_steps(part):
         steps = [functools.partial(rs_start, part, 0)]
@@ -599,7 +661,7 @@
         g2 = two_heads(dah[b, chunk_rows(c)])
         low = probs[i]
         prob = low.astype(F32)
-        d_prob = dot_nt(g2, slots[c, pairs + b])
+        d_prob = dot_nt(g2, slots[c, value_at + b])
         weighted = prob * d_prob
         d_score = (weighted - prob * jnp.sum(weighted, axis=1, keepdims=True)).astype(BF16)
         d_query = merge_heads(dot(d_score, slots[c, b])) * (1.0 / math.sqrt(HEAD_DIM))
@@ -638,7 +700,7 @@
             far = far + dslots[c, b, plan.far_slot :]
         back = dot_tn(select, far.astype(BF16))
         for s in range(seq):
-            fsend[s, b] = back[s * NR : (s + 1) * NR].astype(BF16)
+            fsend[s, b] = back[s * far_rows : (s + 1) * far_rows].astype(BF16)
         return carry
 
     own_done = []
@@ -658,16 +720,12 @@
 
     lax.fori_loop(0, blocks, fold, 0)
 
-    def far_back(k):
-        other, device = peer(3, k)
-        return remote(
-            fsend.at[other], frecv.at[k - 1], fback_send.at[k - 1], fback_recv.at[k - 1], device
-        )
-
-    halo_start(hsend, hrecv, back_send, back_recv)
-    for k in range(1, seq):
-        far_back(k).start()
-
+    back_halo = Halo(hsend, hrecv, back_send, back_recv)
+    back_far = Far(
+        lambda other: fsend.at[other], lambda k: frecv.at[k - 1], fback_send, fback_recv
+    )
+    back_far.start()
+    back_halo.start()
     advance("fold")
 
     d_query = dq[...]
@@ -679,9 +737,8 @@
     rs_start(2 * tiles + 1, 0)
     advance("q")
 
-    halo_wait(hsend, hrecv, back_send, back_recv)
-    for k in range(1, seq):
-        far_back(k).wait()
+    back_halo.wait()
+    back_far.wait()
     for lv in range(near + 1):
         at, n = level_start(lv), span >> lv
         lo, hi = lv * NR, (lv + 1) * NR
@@ -690,10 +747,11 @@
     far_sum = fsend[seq_id].astype(F32)
     for k in range(1, seq):
         far_sum = far_sum + frecv[k - 1].astype(F32)
+    coarse[far_at:] = jnp.zeros((plan.coarse_rows - far_at, 2 * width), BF16)
     for b in range(blocks):
         cols = slice(b * LANES, (b + 1) * LANES)
         coarse[:far_at, cols] = own[b, span : span + far_at].astype(BF16)
-        coarse[far_at:, cols] = far_sum[b].astype(BF16)
+        coarse[far_at : far_at + far_rows, cols] = far_sum[b].astype(BF16)
     for half in range(2):
         passed = dot(spread[...], coarse[:, half * width : (half + 1) * width])
         for b in range(pairs):
@@ -731,7 +789,7 @@
 
     def vec_finish(digit):
         for k in range(1, count[digit]):
-            vec_copy(digit, k).wait_recv()
+            vec_copy(digit, k).wait()
         acc = jnp.zeros((VEC_ROWS, width), F32)
         for s in range(count[digit]):
             acc = acc + jnp.where(index[digit] == s, vstage[digit], vec_received[digit][s])
@@ -742,16 +800,6 @@
 
     vec_start(0)
     advance("ln1")
-
-    for part in range(len(plan.parts)):
-        for digit in range(4):
-            for k in range(1, count[digit]):
-                rs_copy(part, digit, k).wait_send()
-                if digit < 3 or plan.scatter:
-                    ag_copy(part, digit, k).wait_send()
-    for digit in range(4):
-        for k in range(1, count[digit]):
-            vec_copy(digit, k).wait_send()
 
 
 def unpack_kernel(
@@ -837,7 +885,8 @@
         pltpu.VMEM((2 * pairs + 1, span + plan.far_row, LANES), BF16),
         pltpu.VMEM((2, 2 * pairs + 1, plan.edge, LANES), BF16),
         pltpu.VMEM((2, 2 * pairs + 1, plan.edge, LANES), BF16),
-        pltpu.VMEM((seq, NR, 2 * width + LANES), BF16),
+        pltpu.VMEM((seq, plan.far_rows, width + LANES), BF16),
+        pltpu.VMEM((seq, plan.far_rows, width), BF16),
         pltpu.VMEM((plan.chunks, 2 * pairs + 1, plan.slots, LANES), BF16),
         pltpu.VMEM((plan.chunks, plan.chunk, plan.slots), F32),
         pltpu.VMEM((items, 2 * plan.chunk, plan.slots), BF16),
@@ -845,8 +894,8 @@
         pltpu.VMEM((2 * pairs, span + plan.far_row, LANES), F32),
         pltpu.VMEM((2, 2 * pairs, plan.edge, LANES), BF16),
         pltpu.VMEM((2, 2 * pairs, plan.edge, LANES), BF16),
-        pltpu.VMEM((seq, 2 * pairs, NR, LANES), BF16),
-        pltpu.VMEM((seq - 1, 2 * pairs, NR, LANES), BF16),
+        pltpu.VMEM((seq, 2 * pairs, plan.far_rows, LANES), BF16),
+        pltpu.VMEM((seq - 1, 2 * pairs, plan.far_rows, LANES), BF16),
         pltpu.VMEM((plan.coarse_rows, 2 * width), BF16),
         pltpu.VMEM((span, plan.coarse_rows), BF16),
         pltpu.VMEM((span, 2 * width), BF16),
@@ -863,8 +912,8 @@
         pltpu.VMEM((2, span, LANES), F32),
         pltpu.VMEM((tiles, width), F32),
         dma((7 + tiles,)),
-        dma((2,)), dma((2,)),
-        dma((seq - 1,)), dma((seq - 1,)),
+        dma((2, 2)), dma((2, 2)),
+        dma((2, seq - 1)), dma((2, seq - 1)),
         dma((2,)), dma((2,)),
         dma((seq - 1,)), dma((seq - 1,)),
         dma((n_parts, 4, most)), dma((n_parts, 4, most)),

time: 102 us -> 97.1 us (0.952)
  Pallas kernels: 101 us -> 96.3 us
    pallas_call x1, Pallas kernels: 95.9 us -> 90.7 us  [shards(): pl.pallas_call(functools.partial(layer_kernel, plan), out_shape=(pltpu.VM...]
where the time goes in v5:
time: 97.1 us; the launch traced here: 96.9 us
  Pallas kernels  96.3 us (99%)
    pallas_call x1, Pallas kernels, shards(): pl.pallas_call(functools.partial(layer_kernel, plan), out_shape=(pltpu.VM...  90.7 us
    pallas_call x1, Pallas kernels, shards(): pl.pallas_call(functools.partial(unpack_kernel, width, tiles), out_shape=...  5.55 us

profile of v5, /device:TPU:0, one launch (start us, length us, event | category | flops | bytes accessed | tf_op | source)
XLA Modules:
  0.0 96.9 jit_solution(16685636840233930800)
XLA Ops:
  0.7 90.7 %layer.1 = (bf16[1,256,512]{2,1,0:T(8,128)(2,1)S(1)}, bf16[1,256,512]{2,1,0:T(8,128)(2,1)S(1)}, bf16[6144,512]{1,0:T(8,128)(2,1)S(1)}, f32[16,512]{1,0:T(8,128)S(1)}) custom-call(bf16[1,256,512]{2,1,0:T(8,128)(2,1)} %tok_hbm.1, s32[1,256]{1,0:T(1,128)} %ids_ref.1, f32[512]{0:T(512)} %preg_ref.1, f32[512]{0:T(512)} %pres_ref.1, bf16[512,512]{1,0:T(8,128)(2,1)} %wq_hbm.1, ...), custom_call_target="tpu_custom_call" | custom-call | tf_op jit(solution)/shard_map/layer/pallas_call | solution.py:923
  91.4 5.5 %unpack.1 = (f32[512,512]{1,0:T(8,128)}, f32[512,512]{1,0:T(8,128)}, f32[512,512]{1,0:T(8,128)}, f32[512,512]{1,0:T(8,128)}, f32[512,2048]{1,0:T(8,128)}, /*inde...) custom-call(bf16[6144,512]{1,0:T(8,128)(2,1)S(1)} %get-tuple-element, ...), custom_call_target="tpu_custom_call" | custom-call | tf_op jit(solution)/shard_map/unpack/pallas_call | solution.py:948

commit v6 on v5

--- a/solution.py
+++ b/solution.py
@@ -48,22 +48,22 @@
 
 
 ORDER = {
-    "f2": [0, 1],
-    "f3": [2, 3],
-    "ln2": [4],
-    "b0": [5],
-    "b1": [0, 6],
-    "b2": [1, 7, 8],
-    "b4": [2],
-    "b6": [0],
-    "b7": [3, 1],
-    "fold": [2],
-    "q": [4, 0, 3, 1, 5, 9, 4, 6, 5, 7],
+    "f1": [0],
+    "f2": [1, 2],
+    "f3": [3, 4, 5],
+    "ln2": [0],
+    "b0": [6, 7],
+    "b1": [1, 8],
+    "b3": [2],
+    "b5": [0],
+    "b6": [3],
+    "b7": [1],
+    "fold": [2, 4],
+    "q": [3, 5, 9, 0, 6, 1, 4, 7, 5, 6, 8],
     "ln1": [
-        2, 6, 8, 0, 7, 10, 9, 11, 3, 8, 1, 0, 4, -1, 9, 10, 5, 1, 2, 11, 6, 10, 0, -1,
-        7, 2, 3, 0, 11, 1, 8, 4, 1, 2, 3, 9, -1, 4, 5, 2, 6, 3, 10, 5, 3, 7, 4, 6,
-        11, -1, 8, 4, 5, 7, 9, 6, 10, 8, 5, 11, 6, 9, 7, 10, 7, 11, 8, 9, 8, 10, 9, 11,
-        10, 11,
+        2, 7, 9, 10, 3, 11, 8, 0, 9, 1, 4, 10, -1, 5, 0, 11, 6, 1, 10, 2, -1, 7, 0, 11,
+        3, 0, 8, 2, 1, 9, 1, 3, -1, 4, 5, 2, 6, 2, 10, 4, 3, 5, 7, 3, 6, 11, -1, 8,
+        4, 9, 7, 4, 5, 10, 5, 8, 11, 6, 9, 6, 10, 7, 11, 7, 8, 9, 8, 10, 9, 11, 10, 11,
     ],
 }
 

time: 97.1 us -> 95 us (0.978)
  Pallas kernels: 96.3 us -> 94.1 us
    pallas_call x1, Pallas kernels: 90.7 us -> 88.5 us  [shards(): pl.pallas_call(functools.partial(layer_kernel, plan), out_shape=(pltpu.VM...]
where the time goes in v6:
time: 95 us; the launch traced here: 94.8 us
  Pallas kernels  94.1 us (99%)
    pallas_call x1, Pallas kernels, shards(): pl.pallas_call(functools.partial(layer_kernel, plan), out_shape=(pltpu.VM...  88.5 us
    pallas_call x1, Pallas kernels, shards(): pl.pallas_call(functools.partial(unpack_kernel, width, tiles), out_shape=...  5.55 us

profile of v6, /device:TPU:0, one launch (start us, length us, event | category | flops | bytes accessed | tf_op | source)
XLA Modules:
  0.0 94.8 jit_solution(11268321022707774922)
XLA Ops:
  0.7 88.5 %layer.1 = (bf16[1,256,512]{2,1,0:T(8,128)(2,1)S(1)}, bf16[1,256,512]{2,1,0:T(8,128)(2,1)S(1)}, bf16[6144,512]{1,0:T(8,128)(2,1)S(1)}, f32[16,512]{1,0:T(8,128)S(1)}) custom-call(bf16[1,256,512]{2,1,0:T(8,128)(2,1)} %tok_hbm.1, s32[1,256]{1,0:T(1,128)} %ids_ref.1, f32[512]{0:T(512)} %preg_ref.1, f32[512]{0:T(512)} %pres_ref.1, bf16[512,512]{1,0:T(8,128)(2,1)} %wq_hbm.1, ...), custom_call_target="tpu_custom_call" | custom-call | tf_op jit(solution)/shard_map/layer/pallas_call | solution.py:923
  89.2 5.5 %unpack.1 = (f32[512,512]{1,0:T(8,128)}, f32[512,512]{1,0:T(8,128)}, f32[512,512]{1,0:T(8,128)}, f32[512,512]{1,0:T(8,128)}, f32[512,2048]{1,0:T(8,128)}, /*inde...) custom-call(bf16[6144,512]{1,0:T(8,128)(2,1)S(1)} %get-tuple-element, ...), custom_call_target="tpu_custom_call" | custom-call | tf_op jit(solution)/shard_map/unpack/pallas_call | solution.py:948
